TPU v7x, 32 devices: a whole 2x2x4 slice. The times are simulated.
32 devices in a mesh: tp: 4 (over z), dp: 8 (over y, x, core).
Axes of the slice: x: 2, y: 2, z: 4, core: 2. Of those that a mesh axis runs over, the one named last changes fastest.
Arguments:
- design: float32 [49152, 2560], P('dp', 'tp')
- target: float32 [49152], P('dp')
- ridge: float32 [], replicated
Outputs:
- output 1: float32 [2560], replicated
- output 2: float32 [49152], P('dp')
All inputs are finite; a program needn't handle non-finite values.
Results may differ from a plain program's by a relative error of at most 0.001.
Values sent between devices are 32-bit elements.
A program may use at most 1 GiB of HBM per device.

v0:
```python
import functools

import jax
import jax.numpy as jnp
from jax import lax
from jax.experimental import pallas as pl
from jax.experimental.pallas import tpu as pltpu
from jax.sharding import PartitionSpec as P


LANES = 128
SUB = 8
BLK = 128
NB = 512
CHUNKS = 5
MESH = pl.DeviceIdType.MESH
F32 = jnp.float32
BF16 = jnp.bfloat16


def split3(x):
    hi = x.astype(BF16)
    rest = x - hi.astype(F32)
    mid = rest.astype(BF16)
    low = (rest - mid.astype(F32)).astype(BF16)
    return hi, mid, low


def lhs_cat(x):
    hi, mid, low = split3(x)
    return jnp.concatenate([hi, mid, hi, low, mid, hi], axis=1)


def rhs_cat(x):
    hi, mid, low = split3(x)
    return jnp.concatenate([mid, hi, low, hi, mid, hi], axis=0)


def dot_cat(lhs, rhs):
    return lax.dot_general(lhs, rhs, (((1,), (0,)), ((), ())), preferred_element_type=F32)


def row_sums(parts, sub):
    for shift in (4, 2, 1):
        low = (sub & shift) == 0
        nxt = []
        for t in range(shift):
            a, b = parts[t], parts[t + shift]
            keep = jnp.where(low, a, b)
            move = jnp.where(low, b, a)
            nxt.append(keep + xor_roll(move, shift, sub))
        parts = nxt
    return parts[0]


def xor_roll(x, shift, sub):
    if shift == 4:
        return pltpu.roll(x, 4, 0)
    low = (sub & shift) == 0
    return jnp.where(low, pltpu.roll(x, SUB - shift, 0), pltpu.roll(x, shift, 0))


def bcast_lane(x, c):
    return jnp.broadcast_to(x[:, c:c + 1], (SUB, LANES))


def bcast_row(x, p):
    return jnp.broadcast_to(x[p:p + 1, :], (SUB, LANES))


def factor_block(load, sub, lane):
    octs = BLK // SUB
    a = [load(o) for o in range(octs)]
    e = [jnp.where(lane == sub + SUB * o, 1.0, 0.0).astype(F32) for o in range(octs)]
    out = [None] * octs
    for t in range(octs // 2):
        o0, o1 = 2 * t, 2 * t + 1
        c0 = 16 * t
        r0, r1, e0, e1 = a[o0], a[o1], e[o0], e[o1]
        b0 = [bcast_lane(r0, c0 + q) for q in range(16)]
        b1 = [bcast_lane(r1, c0 + q) for q in range(16)]
        d0 = jnp.ones((SUB, LANES), F32)
        d1 = jnp.ones((SUB, LANES), F32)
        for p in range(16):
            ps = p % 8
            first = p < 8
            piv = bcast_row(b0[p] if first else b1[p], ps)
            inv = 1.0 / piv
            if first:
                d0 = jnp.where(sub == ps, piv, d0)
                m0 = jnp.where(sub > ps, b0[p] * inv, 0.0)
                m1 = b1[p] * inv
            else:
                d1 = jnp.where(sub == ps, piv, d1)
                m1 = jnp.where(sub > ps, b1[p] * inv, 0.0)
            for q in range(p + 1, 16):
                row = bcast_row(b0[q] if first else b1[q], ps)
                if first and ps < 7:
                    b0[q] = b0[q] - m0 * row
                b1[q] = b1[q] - m1 * row
            rr, re = bcast_row(r0 if first else r1, ps), bcast_row(e0 if first else e1, ps)
            if first and ps < 7:
                r0 = r0 - m0 * rr
                e0 = e0 - m0 * re
            r1 = r1 - m1 * rr
            e1 = e1 - m1 * re
        s0, s1 = lax.rsqrt(d0), lax.rsqrt(d1)
        u0, u1, v0, v1 = r0 * s0, r1 * s1, e0 * s0, e1 * s1
        out[o0], out[o1] = v0, v1
        for o in range(2 * t + 2, octs):
            xs, ys = [], []
            for k in range(SUB):
                i = SUB * o + k
                g0, g1 = bcast_lane(u0, i), bcast_lane(u1, i)
                xs.append(g0 * u0 + g1 * u1)
                ys.append(g0 * v0 + g1 * v1)
            a[o] = a[o] - row_sums(xs, sub)
            e[o] = e[o] - row_sums(ys, sub)
    return out


def diag_kernel(lam_ref, s_ref, w_ref, work):
    n = s_ref.shape[0]
    steps = n // BLK
    sub = lax.broadcasted_iota(jnp.int32, (SUB, LANES), 0)
    lane = lax.broadcasted_iota(jnp.int32, (SUB, LANES), 1)
    row = lax.broadcasted_iota(jnp.int32, (n, n), 0)
    col = lax.broadcasted_iota(jnp.int32, (n, n), 1)
    work[:, :n] = s_ref[...] + jnp.where(row == col, lam_ref[0], 0.0)
    work[:, n:] = jnp.where(row == col, 1.0, 0.0)

    def step(k, carry):
        base = pl.multiple_of(k * BLK, BLK)
        win = pl.ds(pl.multiple_of(base + BLK, BLK), n)
        diag = pl.ds(base, BLK)

        def load(o):
            return work[pl.ds(pl.multiple_of(base + SUB * o, SUB), SUB), diag]

        inv = jnp.concatenate(factor_block(load, sub, lane), axis=0)
        panel = dot_cat(lhs_cat(inv), rhs_cat(work[diag, win]))
        work[diag, win] = panel
        right = rhs_cat(panel)
        for j in range(steps - 1):
            @pl.when(k == j)
            def _(j=j):
                rows = n - BLK * (j + 1)
                left = lhs_cat(panel[:, :rows].T)
                w = (pl.ds(BLK * (j + 1), rows), pl.ds(BLK * (j + 1), n))
                work[w] = work[w] - dot_cat(left, right)
        return carry

    lax.fori_loop(0, steps, step, 0)
    w_ref[...] = work[:, n:]


def diag_inverse(sdiag, lam):
    n = sdiag.shape[0]
    return pl.pallas_call(
        diag_kernel,
        out_shape=jax.ShapeDtypeStruct((n, n), F32),
        in_specs=[pl.BlockSpec(memory_space=pltpu.SMEM), pl.BlockSpec(memory_space=pltpu.VMEM)],
        out_specs=pl.BlockSpec(memory_space=pltpu.VMEM),
        scratch_shapes=[pltpu.VMEM((n, 2 * n), F32)],
        cost_estimate=pl.CostEstimate(flops=20_000_000_000, bytes_accessed=8 * n * n, transcendentals=0),
        name="diag_inverse",
    )(lam.reshape(1), sdiag)


def finish_kernel(ways, h_ref, b_ref, a_hbm, *refs):
    n, pairs = CHUNKS, [(j, c) for c in range(CHUNKS) for j in range(c)]
    blocks = len(pairs) + n
    hbm = refs[:blocks]
    x_ref, r_ref, near, a_ref, fit, load_sem, a_sem, send_sem, recv_sem = refs[blocks:]
    nb = near.shape[1]
    rows_dev = a_ref.shape[0]
    loads = [pltpu.make_async_copy(ref, near.at[i], load_sem.at[i]) for i, ref in enumerate(hbm)]
    quarter = rows_dev // a_sem.shape[0]
    spans = [pl.ds(quarter * i, quarter) for i in range(a_sem.shape[0])]
    fetch = [pltpu.make_async_copy(a_hbm.at[span], a_ref.at[span], a_sem.at[i]) for i, span in enumerate(spans)]
    order = [pairs.index((j, c)) if j < c else len(pairs) + c for c in range(n) for j in range(c + 1)]
    for i in order:
        loads[i].start()
    for copy in fetch:
        copy.start()
    z = lax.axis_index("tp")
    barrier = pltpu.get_barrier_semaphore()
    for m in range(1, ways):
        pl.semaphore_signal(barrier, inc=1, device_id={"tp": z ^ m}, device_id_type=MESH)
    pl.semaphore_wait(barrier, ways - 1)

    def upper(j, c):
        return near[pairs.index((j, c))]

    half = []
    for c in range(n):
        right = h_ref[c:c + 1, :]
        for j in range(c):
            loads[pairs.index((j, c))].wait()
            right = right - jnp.sum(upper(j, c) * half[j], axis=0, keepdims=True)
        loads[len(pairs) + c].wait()
        half.append(jnp.sum(near[len(pairs) + c] * right, axis=1, keepdims=True))
    for c in reversed(range(n)):
        left = half[c]
        for k in range(c + 1, n):
            left = left - jnp.sum(upper(c, k) * x_ref[k:k + 1, :], axis=1, keepdims=True)
        x_ref[c:c + 1, :] = jnp.sum(near[len(pairs) + c] * left, axis=0, keepdims=True)

    width = nb // ways
    lanes = pl.ds(pl.multiple_of(z * width, LANES), width)
    mine = [x_ref[c:c + 1, lanes] for c in range(n)]

    def product(i, carry):
        rows = pl.ds(pl.multiple_of(i * BLK, BLK), BLK)
        terms = [a_ref[rows, width * c:width * (c + 1)] * mine[c] for c in range(n)]
        total = terms[0]
        for term in terms[1:]:
            total = total + term
        fit[z, pl.ds(i, 1), :] = jnp.sum(total.T, axis=0, keepdims=True)
        return carry

    for i, copy in enumerate(fetch):
        copy.wait()
        lax.fori_loop(quarter // BLK * i, quarter // BLK * (i + 1), product, 0)
    copies = [
        pltpu.make_async_remote_copy(
            src_ref=fit.at[z], dst_ref=fit.at[z], send_sem=send_sem.at[m - 1], recv_sem=recv_sem.at[m - 1],
            device_id={"tp": z ^ m}, device_id_type=MESH)
        for m in range(1, ways)
    ]
    for copy in copies:
        copy.start()
    for copy in copies:
        copy.wait()
    total = fit[0]
    for t in range(1, ways):
        total = total + fit[t]
    r_ref[...] = b_ref[...] - total


def finish(moment, target_blk, design_blk, uppers, inverses, ways):
    blocks = [uppers[j, c] for c in range(CHUNKS) for j in range(c)] + inverses
    rows_dev, cols_dev = design_blk.shape
    vmem, hbm = pl.BlockSpec(memory_space=pltpu.VMEM), pl.BlockSpec(memory_space=pl.ANY)
    return pl.pallas_call(
        functools.partial(finish_kernel, ways),
        out_shape=(jax.ShapeDtypeStruct((CHUNKS, NB), F32), jax.ShapeDtypeStruct((rows_dev // LANES, LANES), F32)),
        in_specs=[vmem, vmem, hbm] + [hbm] * len(blocks),
        out_specs=(vmem, vmem),
        scratch_shapes=[
            pltpu.VMEM((len(blocks), NB, NB), F32),
            pltpu.VMEM((rows_dev, cols_dev), F32),
            pltpu.VMEM((ways, rows_dev // LANES, LANES), F32),
            pltpu.SemaphoreType.DMA((len(blocks),)),
            pltpu.SemaphoreType.DMA((4,)),
            pltpu.SemaphoreType.DMA((ways - 1,)),
            pltpu.SemaphoreType.DMA((ways - 1,)),
        ],
        compiler_params=pltpu.CompilerParams(collective_id=1, has_side_effects=True, vmem_limit_bytes=48 * 1024 * 1024),
        cost_estimate=pl.CostEstimate(flops=5_000_000_000, bytes_accessed=32_000_000, transcendentals=0),
        name="finish",
    )(moment, target_blk.reshape(-1, LANES), design_blk, *blocks)


HIGHEST = lax.Precision.HIGHEST
CONTRACT_ROWS = (((0,), (0,)), ((), ()))


def gram(left, right):
    return lax.dot_general(left, right, CONTRACT_ROWS, precision=HIGHEST, preferred_element_type=F32)


PIECES = 3
AHEAD = 2
SUMMED = ((0, 3), (3, 3), (6, 4))
OUTS = 11
WHEN = ((5, 6, 7, 9, 11, 12, 13), (8, 9, 10, 12, 14, 15, 16), (11, 12, 13, 15, 16, 17, 18))


def ladder(tp_ways, dp_ways):
    return (("dp", 2, 1), ("dp", dp_ways // 2, 2), ("tp", tp_ways, 1))


def place(level):
    axis, ways, dist = level
    return lax.rem(lax.axis_index(axis) // dist, ways)


def member(level, m):
    axis, _, dist = level
    return {axis: lax.axis_index(axis) ^ (m * dist)}


def sweep_kernel(levels, a_ref, b_ref, *refs):
    outs, (p_ref, x_ref, right, moment, got0, got1, got2, swap_send, swap_recv, own_sem, send_sem, recv_sem, free_sem, out_sem) = refs[:OUTS], refs[OUTS:]
    ways = levels[2][1]
    sub_rows = a_ref.shape[0] // ways
    width = a_ref.shape[1] // CHUNKS
    piece = sub_rows // PIECES
    steps = CHUNKS * PIECES
    z = lax.axis_index("tp")
    got = (got0, got1, got2)

    barrier = pltpu.get_barrier_semaphore()
    count = 0
    for level in levels:
        for m in range(1, level[1]):
            pl.semaphore_signal(barrier, inc=1, device_id=member(level, m), device_id_type=MESH)
            count += 1
    pl.semaphore_wait(barrier, count)

    def own(c):
        return pltpu.make_async_copy(
            a_ref.at[pl.ds(z * sub_rows, sub_rows), pl.ds(width * c, width)], x_ref.at[c, z], own_sem.at[c])

    def travel(p, m):
        c, r = p // PIECES, lax.rem(p, PIECES)
        rows = pl.ds(pl.multiple_of((z ^ m) * sub_rows + r * piece, SUB), piece)
        cols = pl.ds(pl.multiple_of(c * width, LANES), width)
        return pltpu.make_async_remote_copy(
            src_ref=a_ref.at[rows, cols],
            dst_ref=x_ref.at[c, z, pl.ds(pl.multiple_of(r * piece, SUB), piece)],
            send_sem=swap_send.at[p, m - 1],
            recv_sem=swap_recv.at[p, m - 1],
            device_id=member(levels[2], m),
            device_id_type=MESH,
        )

    def load(c, r):
        rows = pl.ds(pl.multiple_of(r * piece, SUB), piece)
        return jnp.concatenate([x_ref[c, t, rows, :] for t in range(ways)], axis=1)

    def span(g, depth):
        first, n = SUMMED[g]
        start, rows = first * NB, n * NB
        for level in levels[:depth]:
            rows //= level[1]
            start = start + place(level) * rows
        return start, rows

    def part(g, depth, m):
        start, _ = span(g, depth)
        rows = span(g, depth + 1)[1]
        return pl.ds(pl.multiple_of(start + (place(levels[depth]) ^ m) * rows, SUB), rows)

    base = [sum(level[1] - 1 for level in levels[:d]) for d in range(3)]

    def scatter(g, depth, m):
        i = base[depth] + m - 1
        return pltpu.make_async_remote_copy(
            src_ref=p_ref.at[part(g, depth, m)],
            dst_ref=slot(g, depth, m),
            send_sem=send_sem.at[g, 0, i],
            recv_sem=recv_sem.at[g, 0, i],
            device_id=member(levels[depth], m),
            device_id_type=MESH,
        )

    def slot(g, depth, m):
        n = SUMMED[g][1] * NB
        at, rows = 0, n
        for d, level in enumerate(levels[:depth + 1]):
            rows //= level[1]
            if d < depth:
                at += rows * (level[1] - 1)
        return got[g].at[pl.ds(at + rows * (m - 1), rows)]

    def gather(g, depth, m):
        i = base[depth] + m - 1
        return pltpu.make_async_remote_copy(
            src_ref=p_ref.at[part(g, depth, 0)],
            dst_ref=p_ref.at[part(g, depth, 0)],
            send_sem=send_sem.at[g, 1, i],
            recv_sem=recv_sem.at[g, 1, i],
            device_id=member(levels[depth], m),
            device_id_type=MESH,
        )

    def start(kind, g, depth):
        if kind is gather:
            pl.semaphore_wait(free_sem.at[g, depth], levels[depth][1] - 1)
        for m in range(1, levels[depth][1]):
            kind(g, depth, m).start()

    def finish(kind, g, depth):
        for m in range(1, levels[depth][1]):
            kind(g, depth, m).wait()
        if kind is scatter:
            for m in range(1, levels[depth][1]):
                pl.semaphore_signal(free_sem.at[g, depth], inc=1, device_id=member(levels[depth], m), device_id_type=MESH)
            rows = part(g, depth, 0)
            total = p_ref[rows]
            for m in range(1, levels[depth][1]):
                total = total + slot(g, depth, m)[...]
            p_ref[rows] = total

    def stage(g, s):
        order = [(scatter, 0), (scatter, 1), (scatter, 2), (gather, 2), (gather, 1), (gather, 0)]
        if s > 0:
            kind, depth = order[s - 1]
            finish(kind, g, depth)
        if s < len(order):
            kind, depth = order[s]
            start(kind, g, depth)
        else:
            first, n = SUMMED[g]
            for i in range(first, first + n):
                leave(i).start()

    def leave(i):
        rows = pl.ds(NB * i, NB) if i < OUTS - 1 else pl.ds(NB * i, p_ref.shape[0] - NB * i)
        return pltpu.make_async_copy(p_ref.at[rows], outs[i], out_sem.at[i])

    def stages(p, first):
        for g, when in enumerate(WHEN):
            for s, w in enumerate(when):
                if w < steps and (s == 0) == first:
                    @pl.when(p == w)
                    def _(g=g, s=s):
                        stage(g, s)

    for c in range(CHUNKS):
        own(c).start()
    for p in range(AHEAD):
        for m in range(1, ways):
            travel(p, m).start()

    def step(p, carry):
        c, r = p // PIECES, lax.rem(p, PIECES)
        for m in range(1, ways):
            travel(p, m).wait()

        @pl.when(p + AHEAD < steps)
        def _():
            for m in range(1, ways):
                travel(p + AHEAD, m).start()

        @pl.when(r == 0)
        def _():
            own(c).wait()
            moment[...] = jnp.zeros_like(moment)

        stages(p, False)
        new = load(c, r)
        for i, x in enumerate(split3(new)):
            right[i] = x
        weight = b_ref[pl.ds(pl.multiple_of(r * piece, SUB), piece), :]
        moment[...] += jnp.sum(new * weight, axis=0, keepdims=True)
        corner = lax.div(c * (c + 1), 2)

        def product(j, inner):
            left = split3(load(j, r).T)
            total = None
            for a, b in ((0, 2), (2, 0), (1, 1), (0, 1), (1, 0), (0, 0)):
                term = dot_cat(left[a], right[b])
                total = term if total is None else total + term
            rows = pl.ds(pl.multiple_of((corner + j) * NB, NB), NB)

            @pl.when(r == 0)
            def _():
                p_ref[rows] = total

            @pl.when(r > 0)
            def _():
                p_ref[rows] = p_ref[rows] + total

            return inner

        lax.fori_loop(0, c + 1, product, 0)

        @pl.when(r == PIECES - 1)
        def _():
            last = (corner + c + 1) * NB - SUB
            rows = pl.ds(pl.multiple_of(last, SUB), SUB)
            half = NB // 2
            tail = p_ref[rows, :half]
            row = lax.broadcasted_iota(jnp.int32, tail.shape, 0)
            tail = jnp.where(row == SUB - 2, moment[:, :half], tail)
            p_ref[rows, :half] = jnp.where(row == SUB - 1, moment[:, half:], tail)

        stages(p, True)
        return carry

    lax.fori_loop(0, steps, step, 0)
    leave(OUTS - 1).start()
    for p in range(steps, max(WHEN[-1]) + 1):
        for g, when in enumerate(WHEN):
            for s, w in enumerate(when):
                if w == p:
                    stage(g, s)
    for i in range(OUTS):
        leave(i).wait()


def sweep(design_blk, target_col, tp_ways, dp_ways):
    levels = ladder(tp_ways, dp_ways)
    sub_rows = design_blk.shape[0] // tp_ways
    piece = sub_rows // PIECES
    blocks = CHUNKS * (CHUNKS + 1) // 2
    steps = CHUNKS * PIECES
    peers = sum(level[1] - 1 for level in levels)

    def landing(n):
        rows, total = n * NB, 0
        for level in levels:
            rows //= level[1]
            total += rows * (level[1] - 1)
        return pltpu.VMEM((total, NB), F32)

    return pl.pallas_call(
        functools.partial(sweep_kernel, levels),
        out_shape=[jax.ShapeDtypeStruct((NB, NB), F32)] * (OUTS - 1) + [jax.ShapeDtypeStruct((CHUNKS * NB, NB), F32)],
        in_specs=[pl.BlockSpec(memory_space=pl.ANY), pl.BlockSpec(memory_space=pltpu.VMEM)],
        out_specs=[pl.BlockSpec(memory_space=pl.ANY)] * OUTS,
        scratch_shapes=[
            pltpu.VMEM((blocks * NB, NB), F32),
            pltpu.VMEM((CHUNKS, tp_ways, sub_rows, NB // tp_ways), F32),
            pltpu.VMEM((3, piece, NB), BF16),
            pltpu.VMEM((1, NB), F32),
            *(landing(n) for _, n in SUMMED),
            pltpu.SemaphoreType.DMA((steps, tp_ways - 1)),
            pltpu.SemaphoreType.DMA((steps, tp_ways - 1)),
            pltpu.SemaphoreType.DMA((CHUNKS,)),
            pltpu.SemaphoreType.DMA((len(SUMMED), 2, peers)),
            pltpu.SemaphoreType.DMA((len(SUMMED), 2, peers)),
            pltpu.SemaphoreType.REGULAR((len(SUMMED), len(levels))),
            pltpu.SemaphoreType.DMA((OUTS,)),
        ],
        compiler_params=pltpu.CompilerParams(collective_id=0, has_side_effects=True, vmem_limit_bytes=60 * 1024 * 1024),
        cost_estimate=pl.CostEstimate(flops=300_000_000_000, bytes_accessed=32_000_000, transcendentals=0),
        name="sweep",
    )(design_blk, target_col)


def swap(x, axis, ways, mask):
    return lax.ppermute(x, axis, [(i, i ^ mask) for i in range(ways)])


def pick(stack, i):
    return lax.dynamic_index_in_dim(stack, i, 0, keepdims=False)


def scatter_sum(x, me, ways, send):
    parts = x.reshape(ways, -1, x.shape[1])
    total = pick(parts, me)
    for m in range(1, ways):
        total = total + send(pick(parts, me ^ m), m)
    return total


def gather(x, me, ways, send):
    out = jnp.zeros((ways * x.shape[0], x.shape[1]), x.dtype)
    for m in range(ways):
        out = lax.dynamic_update_slice(out, send(x, m) if m else x, ((me ^ m) * x.shape[0], 0))
    return out


def sum_all(x, tp_ways, dp_ways):
    tp, dp = lax.axis_index('tp'), lax.axis_index('dp')
    core = (dp & 1, 2, lambda v, m: swap(v, 'dp', dp_ways, m))
    plane = (dp >> 1, dp_ways // 2, lambda v, m: swap(v, 'dp', dp_ways, 2 * m))
    column = (tp, tp_ways, lambda v, m: swap(v, 'tp', tp_ways, m))
    for level in (core, plane, column):
        x = scatter_sum(x, *level)
    for level in (column, plane, core):
        x = gather(x, *level)
    return x


def solution(mesh):
    tp_ways, dp_ways = mesh.shape['tp'], mesh.shape['dp']

    def local_fit(design_blk, target_blk, ridge):
        rows_dev, _ = design_blk.shape
        sub_rows = rows_dev // tp_ways
        width = NB // tp_ways
        tp = lax.axis_index('tp')
        target_part = lax.dynamic_slice_in_dim(target_blk, tp * sub_rows, sub_rows)
        *blocks, last = sweep(design_blk, target_part[:, None], tp_ways, dp_ways)
        last = sum_all(last, tp_ways, dp_ways)
        blocks += [last[NB * k:NB * (k + 1)] for k in range(CHUNKS)]

        uppers, inverses, moments = {}, [], []
        for c in range(CHUNKS):
            total = blocks[c * (c + 1) // 2:]
            moments.append(total[c][-2:, :NB // 2].reshape(1, NB))
            for k in range(c + 1):
                block = total[k]
                for j in range(k):
                    block = block - gram(uppers[j, k], uppers[j, c])
                if k < c:
                    uppers[k, c] = jnp.dot(inverses[k], block, precision=HIGHEST, preferred_element_type=F32)
                else:
                    inverses.append(diag_inverse(block, ridge))
        order, residual = finish(jnp.concatenate(moments, axis=0), target_blk, design_blk, uppers, inverses, tp_ways)
        coeffs = order.reshape(CHUNKS, tp_ways, width).transpose(1, 0, 2).reshape(-1)
        return coeffs, residual.reshape(-1)

    return jax.shard_map(local_fit, mesh=mesh, in_specs=(P('dp', 'tp'), P('dp'), P()), out_specs=(P(), P('dp')), check_vma=False)
```

profile of v0, /device:TPU:0, one launch (start us, length us, event | category | flops | bytes accessed | tf_op | source)
XLA Modules:
  0.0 742.0 jit_solution(18264561875835774510)
XLA Ops:
  2.6 440.3 %sweep.1 = (f32[512,512]{1,0:T(8,128)}, f32[512,512]{1,0:T(8,128)}, f32[512,512]{1,0:T(8,128)}, f32[512,512]{1,0:T(8,128)}, f32[512,512]{1,0:T(8,128)}, /*index=...) custom-call(f32[6144,640]{1,0:T(8,128)} %a_hbm.1, ...), custom_call_target="tpu_custom_call" | custom-call | flops 299999985664 | bytes 32000000 | tf_op jit(solution)/shard_map/sweep/pallas_call | solution.py:510
  442.9 3.5 dynamic-slice_bitcast_fusion
  447.5 19.7 %diag_inverse.5.refs_10_ = f32[512,512]{1,0:T(8,128)} custom-call(f32[1]{0:T(128)} %bitcast.114.lam_ref, f32[512,512]{1,0:T(8,128)} %get-tuple-element.15.s_ref), custom_call_target="tpu_custom_call" | custom-call | flops 20000000000 | bytes 2097152 | tf_op jit(solution)/shard_map/diag_inverse/pallas_call | solution.py:159
  467.2 3.2 fusion.21.refs_3_
  477.0 19.9 %diag_inverse.6.refs_11_ = f32[512,512]{1,0:T(8,128)} custom-call(f32[1]{0:T(128)} %bitcast.115.lam_ref, f32[512,512]{1,0:T(8,128)} %convolution_subtract_fusion.9.s_ref), custom_call_target="tpu_custom_call" | custom-call | flops 20000000000 | bytes 2097152 | tf_op jit(solution)/shard_map/diag_inverse/pallas_call | solution.py:159
  496.9 3.2 convolution_subtract_fusion.7
  507.6 3.2 convolution_subtract_fusion.6
  513.7 19.6 %diag_inverse.7.refs_12_ = f32[512,512]{1,0:T(8,128)} custom-call(f32[1]{0:T(128)} %bitcast.116.lam_ref, f32[512,512]{1,0:T(8,128)} %convolution_subtract_fusion.5.s_ref), custom_call_target="tpu_custom_call" | custom-call | flops 20000000000 | bytes 2097152 | tf_op jit(solution)/shard_map/diag_inverse/pallas_call | solution.py:159
  533.3 3.1 bitcast_add_fusion
  542.1 2.9 convolution_subtract_fusion.2
  545.0 9.3 %collective-permute-done.1 = f32[320,512]{1,0:T(8,128)S(1)} collective-permute-done((f32[320,512]{1,0:T(8,128)S(1)}, f32[320,512]{1,0:T(8,128)S(1)}, u32[]{:S(2)}, u32[]{:S(2)}) %collective-permute-start.1) | collective-permute-done | bytes 655392 | tf_op jit(solution)/shard_map/ppermute | solution.py:536
  554.3 13.5 %collective-permute-done.2 = f32[320,512]{1,0:T(8,128)S(1)} collective-permute-done((f32[320,512]{1,0:T(8,128)S(1)}, f32[320,512]{1,0:T(8,128)S(1)}, u32[]{:S(2)}, u32[]{:S(2)}) %collective-permute-start.2) | collective-permute-done | bytes 655392 | tf_op jit(solution)/shard_map/ppermute | solution.py:536
  574.1 2.9 convolution_subtract_fusion.3
  577.2 8.4 %collective-permute-done.5 = f32[80,512]{1,0:T(8,128)} collective-permute-done((f32[80,512]{1,0:T(8,128)}, f32[80,512]{1,0:T(8,128)}, u32[]{:S(2)}, u32[]{:S(2)}) %collective-permute-start.5) | collective-permute-done | bytes 163872 | tf_op jit(solution)/shard_map/ppermute | solution.py:536
  591.8 4.1 convolution_subtract_fusion.1
  598.1 5.8 collective-permute-done.8
  609.5 4.3 fusion.23.refs_5_
  618.1 5.1 collective-permute-done.10
  625.2 9.4 %collective-permute-done.11 = f32[320,512]{1,0:T(8,128)} collective-permute-done((f32[320,512]{1,0:T(8,128)}, f32[320,512]{1,0:T(8,128)}, u32[]{:S(2)}, u32[]{:S(2)}) %collective-permute-start.11) | collective-permute-done | bytes 655392 | tf_op jit(solution)/shard_map/ppermute | solution.py:536
  638.2 4.8 convolution_subtract_fusion.s_ref
  643.0 19.4 %diag_inverse.8.refs_13_ = f32[512,512]{1,0:T(8,128)} custom-call(f32[1]{0:T(128)} %bitcast.117.lam_ref, f32[512,512]{1,0:T(8,128)} %convolution_subtract_fusion.s_ref), custom_call_target="tpu_custom_call" | custom-call | flops 20000000000 | bytes 2097152 | tf_op jit(solution)/shard_map/diag_inverse/pallas_call | solution.py:159
  692.6 3.1 fusion.2.s_ref
  695.7 19.4 %diag_inverse.9.refs_14_ = f32[512,512]{1,0:T(8,128)} custom-call(f32[1]{0:T(128)} %bitcast.118.lam_ref, f32[512,512]{1,0:T(8,128)} %fusion.2.s_ref), custom_call_target="tpu_custom_call" | custom-call | flops 20000000000 | bytes 2097152 | tf_op jit(solution)/shard_map/diag_inverse/pallas_call | solution.py:159
  717.7 22.9 %finish.1 = (f32[5,512]{1,0:T(8,128)S(1)}, f32[48,128]{1,0:T(8,128)S(1)}) custom-call(f32[5,512]{1,0:T(8,128)S(1)} %concatenate.3.h_ref, f32[48,128]{1,0:T(8,128)S(1)} %bitcast.119, f32[6144,640]{1,0:T(8,128)} %a_hbm.1, f32[512,512]{1,0:T(8,128)S(1)} %fusion.18.refs_0_, f32[512,512]{1,0:T(8,128)S(1)} %fusion.19.refs_1_, f32[512,512]{1,0:T(8,128)S(1)} %copy-done.7, ...), custom_call_target="tpu_custom_call" | custom-call | flops 5000000000 | bytes 32000000 | tf_op jit(solution)/shard_map/finish/pallas_call | solution.py:245
  (128 shorter events, 88.6 us)
Async XLA Ops:
  446.5 86.8 %collective-permute-start = (f32[1280,512]{1,0:T(8,128)}, f32[1280,512]{1,0:T(8,128)}, u32[]{:S(2)}, u32[]{:S(2)}) collective-permute-start(f32[1280,512]{1,0:T(8,128)} %dynamic-slice_bitcast_fusion), channel_id=1, source_target_pairs={{0,1},{1,0},{2,3},{3,2},{4,5},{5,4},{6,7},{7,6},{8,9},{9,8},{10,11... | collective-permute-start | bytes 7864328 | tf_op jit(solution)/shard_map/ppermute | solution.py:536
  447.5 19.7 %copy-start.25 = (f32[512,512]{1,0:T(8,128)S(1)}, f32[512,512]{1,0:T(8,128)}, u32[]{:S(2)}) copy-start(f32[512,512]{1,0:T(8,128)} %get-tuple-element.23) | copy-start | bytes 3145732
  467.2 5.1 copy-start.23
  536.6 5.4 copy-start.22
  536.6 17.7 %collective-permute-start.1 = (f32[320,512]{1,0:T(8,128)S(1)}, f32[320,512]{1,0:T(8,128)S(1)}, u32[]{:S(2)}, u32[]{:S(2)}) collective-permute-start(f32[320,512]{1,0:T(8,128)S(1)} %get-tuple-element.30), channel_id=1, source_target_pairs={{0,2},{1,3},{2,0},{3,1},{4,6},{5,7},{6,4},{7,5},{8,10},{9,11},{10,... | collective-permute-start | bytes 1966088 | tf_op jit(solution)/shard_map/ppermute | solution.py:536
  537.3 30.5 %collective-permute-start.2 = (f32[320,512]{1,0:T(8,128)S(1)}, f32[320,512]{1,0:T(8,128)S(1)}, u32[]{:S(2)}, u32[]{:S(2)}) collective-permute-start(f32[320,512]{1,0:T(8,128)S(1)} %get-tuple-element.32), channel_id=1, source_target_pairs={{0,4},{1,5},{2,6},{3,7},{4,0},{5,1},{6,2},{7,3},{8,12},{9,13},{10,... | collective-permute-start | bytes 1966088 | tf_op jit(solution)/shard_map/ppermute | solution.py:536
  538.7 29.1 %collective-permute-start.3 = (f32[320,512]{1,0:T(8,128)S(1)}, f32[320,512]{1,0:T(8,128)S(1)}, u32[]{:S(2)}, u32[]{:S(2)}) collective-permute-start(f32[320,512]{1,0:T(8,128)S(1)} %get-tuple-element.31), channel_id=1, source_target_pairs={{0,6},{1,7},{2,4},{3,5},{4,2},{5,3},{6,0},{7,1},{8,14},{9,15},{10,... | collective-permute-start | bytes 1966088 | tf_op jit(solution)/shard_map/ppermute | solution.py:536
  545.0 29.2 %copy-start = (f32[512,512]{1,0:T(8,128)S(1)}, f32[512,512]{1,0:T(8,128)}, u32[]{:S(2)}) copy-start(f32[512,512]{1,0:T(8,128)} %fusion.22.refs_4_) | copy-start | bytes 3145732
  545.0 29.2 %copy-start.5 = (f32[512,512]{1,0:T(8,128)S(1)}, f32[512,512]{1,0:T(8,128)}, u32[]{:S(2)}) copy-start(f32[512,512]{1,0:T(8,128)} %fusion.20.refs_2_) | copy-start | bytes 3145732
  569.7 7.5 %collective-permute-start.4 = (f32[80,512]{1,0:T(8,128)}, f32[80,512]{1,0:T(8,128)S(1)}, u32[]{:S(2)}, u32[]{:S(2)}) collective-permute-start(f32[80,512]{1,0:T(8,128)} %get-tuple-element.33), channel_id=1, source_target_pairs={{0,8},{8,0},{16,24},{24,16},{1,9},{9,1},{17,25},{25,17},{2,10},{10... | collective-permute-start | bytes 491528 | tf_op jit(solution)/shard_map/ppermute | solution.py:536
  570.9 14.7 %collective-permute-start.5 = (f32[80,512]{1,0:T(8,128)}, f32[80,512]{1,0:T(8,128)}, u32[]{:S(2)}, u32[]{:S(2)}) collective-permute-start(f32[80,512]{1,0:T(8,128)} %get-tuple-element.35), channel_id=1, source_target_pairs={{0,16},{8,24},{16,0},{24,8},{1,17},{9,25},{17,1},{25,9},{2,18},{10... | collective-permute-start | bytes 491528 | tf_op jit(solution)/shard_map/ppermute | solution.py:536
  572.6 13.0 %collective-permute-start.6 = (f32[80,512]{1,0:T(8,128)S(1)}, f32[80,512]{1,0:T(8,128)}, u32[]{:S(2)}, u32[]{:S(2)}) collective-permute-start(f32[80,512]{1,0:T(8,128)S(1)} %get-tuple-element.34), channel_id=1, source_target_pairs={{0,24},{8,16},{16,8},{24,0},{1,25},{9,17},{17,9},{25,1},{2,26},{10... | collective-permute-start | bytes 491528 | tf_op jit(solution)/shard_map/ppermute | solution.py:536
  577.0 14.8 %copy-start.1 = (f32[512,512]{1,0:T(8,128)S(1)}, f32[512,512]{1,0:T(8,128)}, u32[]{:S(2)}) copy-start(f32[512,512]{1,0:T(8,128)} %fusion.22.refs_4_) | copy-start | bytes 3145732
  588.4 9.0 %collective-permute-start.7 = (f32[80,512]{1,0:T(8,128)}, f32[80,512]{1,0:T(8,128)S(1)}, u32[]{:S(2)}, u32[]{:S(2)}) collective-permute-start(f32[80,512]{1,0:T(8,128)} %get-tuple-element.29), channel_id=1, source_target_pairs={{0,8},{8,0},{16,24},{24,16},{1,9},{9,1},{17,25},{25,17},{2,10},{10... | collective-permute-start | bytes 491528 | tf_op jit(solution)/shard_map/ppermute | solution.py:536
  590.8 13.1 %collective-permute-start.8 = (f32[80,512]{1,0:T(8,128)}, f32[80,512]{1,0:T(8,128)S(1)}, u32[]{:S(2)}, u32[]{:S(2)}) collective-permute-start(f32[80,512]{1,0:T(8,128)} %get-tuple-element.29), channel_id=1, source_target_pairs={{0,16},{8,24},{16,0},{24,8},{1,17},{9,25},{17,1},{25,9},{2,18},{10... | collective-permute-start | bytes 491528 | tf_op jit(solution)/shard_map/ppermute | solution.py:536
  595.9 8.7 %collective-permute-start.9 = (f32[80,512]{1,0:T(8,128)}, f32[80,512]{1,0:T(8,128)S(1)}, u32[]{:S(2)}, u32[]{:S(2)}) collective-permute-start(f32[80,512]{1,0:T(8,128)} %get-tuple-element.29), channel_id=1, source_target_pairs={{0,24},{8,16},{16,8},{24,0},{1,25},{9,17},{17,9},{25,1},{2,26},{10... | collective-permute-start | bytes 491528 | tf_op jit(solution)/shard_map/ppermute | solution.py:536
  605.3 17.9 %collective-permute-start.10 = (f32[320,512]{1,0:T(8,128)}, f32[320,512]{1,0:T(8,128)}, u32[]{:S(2)}, u32[]{:S(2)}) collective-permute-start(f32[320,512]{1,0:T(8,128)} %constant_dynamic-update-slice_fusion.6), channel_id=1, source_target_pairs={{0,2},{1,3},{2,0},{3,1},{4,6},{5,7},{6,4},{7,5},{8,10},{9,11},{10,... | collective-permute-start | bytes 1966088 | tf_op jit(solution)/shard_map/ppermute | solution.py:536
  606.9 27.7 %collective-permute-start.11 = (f32[320,512]{1,0:T(8,128)}, f32[320,512]{1,0:T(8,128)}, u32[]{:S(2)}, u32[]{:S(2)}) collective-permute-start(f32[320,512]{1,0:T(8,128)} %constant_dynamic-update-slice_fusion.6), channel_id=1, source_target_pairs={{0,4},{1,5},{2,6},{3,7},{4,0},{5,1},{6,2},{7,3},{8,12},{9,13},{10,... | collective-permute-start | bytes 1966088 | tf_op jit(solution)/shard_map/ppermute | solution.py:536
  608.1 28.5 %collective-permute-start.12 = (f32[320,512]{1,0:T(8,128)}, f32[320,512]{1,0:T(8,128)S(1)}, u32[]{:S(2)}, u32[]{:S(2)}) collective-permute-start(f32[320,512]{1,0:T(8,128)} %constant_dynamic-update-slice_fusion.6), channel_id=1, source_target_pairs={{0,6},{1,7},{2,4},{3,5},{4,2},{5,3},{6,0},{7,1},{8,14},{9,15},{10,... | collective-permute-start | bytes 1966088 | tf_op jit(solution)/shard_map/ppermute | solution.py:536
  637.5 27.7 %collective-permute-start.13 = (f32[1280,512]{1,0:T(8,128)}, f32[1280,512]{1,0:T(8,128)}, u32[]{:S(2)}, u32[]{:S(2)}) collective-permute-start(f32[1280,512]{1,0:T(8,128)} %constant_dynamic-update-slice_fusion.2), channel_id=1, source_target_pairs={{0,1},{1,0},{2,3},{3,2},{4,5},{5,4},{6,7},{7,6},{8,9},{9,8},{10,11... | collective-permute-start | bytes 7864328 | tf_op jit(solution)/shard_map/ppermute | solution.py:536
  669.1 19.3 %copy-start.9 = (f32[512,512]{1,0:T(8,128)}, f32[512,512]{1,0:T(8,128)S(1)}, u32[]{:S(2)}) copy-start(f32[512,512]{1,0:T(8,128)S(1)} %fusion.11.refs_6_) | copy-start | bytes 3145732
  674.8 4.0 copy-start.6
  676.7 9.8 %copy-start.10 = (f32[512,512]{1,0:T(8,128)}, f32[512,512]{1,0:T(8,128)S(1)}, u32[]{:S(2)}) copy-start(f32[512,512]{1,0:T(8,128)S(1)} %fusion.10.refs_7_) | copy-start | bytes 3145732
  695.7 19.5 %copy-start.8 = (f32[6144]{0:T(1024)S(1)}, f32[6144]{0:T(1024)}, u32[]{:S(2)}) copy-start(f32[6144]{0:T(1024)} %param.4) | copy-start | bytes 73732
  (18 other events, 51.1 us)
where the time goes:
time: 749 us; the launch traced here: 742 us
  Pallas kernels  561 us (75%)
  matrix products  75.5 us (10%)
  waiting for transfers between devices  51.9 us (7%)
  local copies, waits for them, and re-layouts  29.4 us (4%)
  starting transfers between devices  16.6 us (2%)
    pallas_call x1, Pallas kernels, sweep(): pl.pallas_call(functools.partial(sweep_kernel, levels), out_shape=[jax.Sh...  440 us
    pallas_call x5, Pallas kernels, diag_inverse(): pl.pallas_call(diag_kernel, out_shape=jax.ShapeDtypeStruct((n, n), F32),...  98 us
    ppermute x14, waiting for transfers between devices, swap(): return lax.ppermute(x, axis, [(i, i ^ mask) for i in range(ways)])  51.9 us
    dot_general x20, matrix products, gram(): lax.dot_general(left, right, CONTRACT_ROWS, precision=HIGHEST, preferred_...  50.8 us
    dot_general x10, matrix products, local_fit(): jnp.dot(inverses[k], block, precision=HIGHEST, preferred_element_type=F32)  24.7 us
    pallas_call x1, Pallas kernels, finish(): pl.pallas_call(functools.partial(finish_kernel, ways), out_shape=(jax.Sha...  22.9 us
    ppermute x14, starting transfers between devices, swap(): return lax.ppermute(x, axis, [(i, i ^ mask) for i in range(ways)])  16.6 us
  transfers between devices with their start and end apart: 14, of which 7 were waited for; matrix products, arithmetic and copies ran while one was open for 8% of the time, Pallas kernels for 11%

commit v1 on v0

--- a/solution.py
+++ b/solution.py
@@ -154,24 +154,25 @@
     w_ref[...] = work[:, n:]
 
 
-def diag_inverse(sdiag, lam):
-    n = sdiag.shape[0]
+def diag_inverse(panel, lam):
+    n = panel.shape[0]
     return pl.pallas_call(
         diag_kernel,
         out_shape=jax.ShapeDtypeStruct((n, n), F32),
-        in_specs=[pl.BlockSpec(memory_space=pltpu.SMEM), pl.BlockSpec(memory_space=pltpu.VMEM)],
-        out_specs=pl.BlockSpec(memory_space=pltpu.VMEM),
+        grid=(1,),
+        in_specs=[pl.BlockSpec(memory_space=pltpu.SMEM), pl.BlockSpec((n, n), lambda i: (0, 0))],
+        out_specs=pl.BlockSpec((n, n), lambda i: (0, 0)),
         scratch_shapes=[pltpu.VMEM((n, 2 * n), F32)],
         cost_estimate=pl.CostEstimate(flops=20_000_000_000, bytes_accessed=8 * n * n, transcendentals=0),
         name="diag_inverse",
-    )(lam.reshape(1), sdiag)
+    )(lam.reshape(1), panel)
 
 
 def finish_kernel(ways, h_ref, b_ref, a_hbm, *refs):
     n, pairs = CHUNKS, [(j, c) for c in range(CHUNKS) for j in range(c)]
-    blocks = len(pairs) + n
-    hbm = refs[:blocks]
-    x_ref, r_ref, near, a_ref, fit, load_sem, a_sem, send_sem, recv_sem = refs[blocks:]
+    panels, tops, inverses, refs = refs[:LAST - 1], refs[LAST - 1:2 * LAST - 1], refs[2 * LAST - 1:3 * LAST], refs[3 * LAST:]
+    x_ref, r_ref, near, a_ref, fit, load_sem, a_sem, send_sem, recv_sem = refs
+    hbm = [tops[j] if c == LAST else panels[j].at[:, pl.ds(NB * (c - j - 1), NB)] for j, c in pairs] + list(inverses)
     nb = near.shape[1]
     rows_dev = a_ref.shape[0]
     loads = [pltpu.make_async_copy(ref, near.at[i], load_sem.at[i]) for i, ref in enumerate(hbm)]
@@ -211,17 +212,20 @@
     mine = [x_ref[c:c + 1, lanes] for c in range(n)]
 
     def product(i, carry):
-        rows = pl.ds(pl.multiple_of(i * BLK, BLK), BLK)
-        terms = [a_ref[rows, width * c:width * (c + 1)] * mine[c] for c in range(n)]
-        total = terms[0]
-        for term in terms[1:]:
-            total = total + term
-        fit[z, pl.ds(i, 1), :] = jnp.sum(total.T, axis=0, keepdims=True)
+        for k in range(group):
+            at = i * group + k
+            rows = pl.ds(pl.multiple_of(at * BLK, BLK), BLK)
+            terms = [a_ref[rows, width * c:width * (c + 1)] * mine[c] for c in range(n)]
+            total = terms[0]
+            for term in terms[1:]:
+                total = total + term
+            fit[z, pl.ds(at, 1), :] = jnp.sum(total.T, axis=0, keepdims=True)
         return carry
 
+    group = 4 if quarter % (4 * BLK) == 0 else 1
     for i, copy in enumerate(fetch):
         copy.wait()
-        lax.fori_loop(quarter // BLK * i, quarter // BLK * (i + 1), product, 0)
+        lax.fori_loop(quarter // (group * BLK) * i, quarter // (group * BLK) * (i + 1), product, 0)
     copies = [
         pltpu.make_async_remote_copy(
             src_ref=fit.at[z], dst_ref=fit.at[z], send_sem=send_sem.at[m - 1], recv_sem=recv_sem.at[m - 1],
@@ -238,20 +242,21 @@
     r_ref[...] = b_ref[...] - total
 
 
-def finish(moment, target_blk, design_blk, uppers, inverses, ways):
-    blocks = [uppers[j, c] for c in range(CHUNKS) for j in range(c)] + inverses
+def finish(moment, target_blk, design_blk, uppers, tops, inverses, ways):
+    blocks = CHUNKS * (CHUNKS + 1) // 2
+    parts = [*uppers, *tops, *inverses]
     rows_dev, cols_dev = design_blk.shape
     vmem, hbm = pl.BlockSpec(memory_space=pltpu.VMEM), pl.BlockSpec(memory_space=pl.ANY)
     return pl.pallas_call(
         functools.partial(finish_kernel, ways),
         out_shape=(jax.ShapeDtypeStruct((CHUNKS, NB), F32), jax.ShapeDtypeStruct((rows_dev // LANES, LANES), F32)),
-        in_specs=[vmem, vmem, hbm] + [hbm] * len(blocks),
+        in_specs=[vmem, vmem, hbm] + [hbm] * len(parts),
         out_specs=(vmem, vmem),
         scratch_shapes=[
-            pltpu.VMEM((len(blocks), NB, NB), F32),
+            pltpu.VMEM((blocks, NB, NB), F32),
             pltpu.VMEM((rows_dev, cols_dev), F32),
             pltpu.VMEM((ways, rows_dev // LANES, LANES), F32),
-            pltpu.SemaphoreType.DMA((len(blocks),)),
+            pltpu.SemaphoreType.DMA((blocks,)),
             pltpu.SemaphoreType.DMA((4,)),
             pltpu.SemaphoreType.DMA((ways - 1,)),
             pltpu.SemaphoreType.DMA((ways - 1,)),
@@ -259,7 +264,7 @@
         compiler_params=pltpu.CompilerParams(collective_id=1, has_side_effects=True, vmem_limit_bytes=48 * 1024 * 1024),
         cost_estimate=pl.CostEstimate(flops=5_000_000_000, bytes_accessed=32_000_000, transcendentals=0),
         name="finish",
-    )(moment, target_blk.reshape(-1, LANES), design_blk, *blocks)
+    )(moment, target_blk.reshape(-1, LANES), design_blk, *parts)
 
 
 HIGHEST = lax.Precision.HIGHEST
@@ -270,15 +275,29 @@
     return lax.dot_general(left, right, CONTRACT_ROWS, precision=HIGHEST, preferred_element_type=F32)
 
 
-PIECES = 3
+PIECES = 6
 AHEAD = 2
-SUMMED = ((0, 3), (3, 3), (6, 4))
-OUTS = 11
-WHEN = ((5, 6, 7, 9, 11, 12, 13), (8, 9, 10, 12, 14, 15, 16), (11, 12, 13, 15, 16, 17, 18))
+LAST = CHUNKS - 1
+PANELS = LAST
+SUMMED = ((0, 3), (3, 3), (6, 4), (10, 5))
+WHEN = (
+    (11, 12, 14, 16, 18, 20, 22, 24, 25),
+    (17, 18, 20, 22, 24, 26, 28, 30, 31),
+    (23, 24, 26, 28, 30, 31, 32, 33, 34),
+    (29, 30),
+)
 
 
 def ladder(tp_ways, dp_ways):
-    return (("dp", 2, 1), ("dp", dp_ways // 2, 2), ("tp", tp_ways, 1))
+    pairs = tuple(("tp", 2, 1 << k) for k in range(tp_ways.bit_length() - 1))
+    return (("dp", 2, 1), ("dp", dp_ways // 2, 2), *pairs)
+
+
+def steps_of(levels, g):
+    if g == len(SUMMED) - 1:
+        return [(False, 0)]
+    depths = range(len(levels))
+    return [(False, d) for d in depths] + [(True, d) for d in reversed(depths)]
 
 
 def place(level):
@@ -291,19 +310,19 @@
     return {axis: lax.axis_index(axis) ^ (m * dist)}
 
 
-def sweep_kernel(levels, a_ref, b_ref, *refs):
-    outs, (p_ref, x_ref, right, moment, got0, got1, got2, swap_send, swap_recv, own_sem, send_sem, recv_sem, free_sem, out_sem) = refs[:OUTS], refs[OUTS:]
-    ways = levels[2][1]
+def sweep_kernel(levels, ways, a_ref, b_ref, *refs):
+    outs, (p_ref, x_ref, right, moment, *got) = refs[:PANELS + 1], refs[PANELS + 1:]
+    swap_send, swap_recv, own_sem, send_sem, recv_sem, free_sem, out_sem = got[len(SUMMED):]
     sub_rows = a_ref.shape[0] // ways
     width = a_ref.shape[1] // CHUNKS
     piece = sub_rows // PIECES
     steps = CHUNKS * PIECES
     z = lax.axis_index("tp")
-    got = (got0, got1, got2)
+    column = ("tp", ways, 1)
 
     barrier = pltpu.get_barrier_semaphore()
     count = 0
-    for level in levels:
+    for level in (*levels[:2], column):
         for m in range(1, level[1]):
             pl.semaphore_signal(barrier, inc=1, device_id=member(level, m), device_id_type=MESH)
             count += 1
@@ -322,7 +341,7 @@
             dst_ref=x_ref.at[c, z, pl.ds(pl.multiple_of(r * piece, SUB), piece)],
             send_sem=swap_send.at[p, m - 1],
             recv_sem=swap_recv.at[p, m - 1],
-            device_id=member(levels[2], m),
+            device_id=member(column, m),
             device_id_type=MESH,
         )
 
@@ -343,7 +362,7 @@
         rows = span(g, depth + 1)[1]
         return pl.ds(pl.multiple_of(start + (place(levels[depth]) ^ m) * rows, SUB), rows)
 
-    base = [sum(level[1] - 1 for level in levels[:d]) for d in range(3)]
+    base = [sum(level[1] - 1 for level in levels[:d]) for d in range(len(levels))]
 
     def scatter(g, depth, m):
         i = base[depth] + m - 1
@@ -376,40 +395,48 @@
             device_id_type=MESH,
         )
 
-    def start(kind, g, depth):
-        if kind is gather:
+    def start(back, g, depth):
+        if back:
             pl.semaphore_wait(free_sem.at[g, depth], levels[depth][1] - 1)
         for m in range(1, levels[depth][1]):
-            kind(g, depth, m).start()
-
-    def finish(kind, g, depth):
-        for m in range(1, levels[depth][1]):
-            kind(g, depth, m).wait()
-        if kind is scatter:
-            for m in range(1, levels[depth][1]):
+            (gather if back else scatter)(g, depth, m).start()
+
+    def finish(back, g, depth):
+        others = range(1, levels[depth][1])
+        for m in others:
+            (gather if back else scatter)(g, depth, m).wait()
+        if back:
+            return
+        if (True, depth) in steps_of(levels, g):
+            for m in others:
                 pl.semaphore_signal(free_sem.at[g, depth], inc=1, device_id=member(levels[depth], m), device_id_type=MESH)
-            rows = part(g, depth, 0)
-            total = p_ref[rows]
-            for m in range(1, levels[depth][1]):
-                total = total + slot(g, depth, m)[...]
-            p_ref[rows] = total
+        rows = part(g, depth, 0)
+        total = p_ref[rows]
+        for m in others:
+            total = total + slot(g, depth, m)[...]
+        p_ref[rows] = total
+
+    def leave(i):
+        c = max(c for c in range(CHUNKS) if c * (c + 1) // 2 <= i)
+        k = i - c * (c + 1) // 2
+        return pltpu.make_async_copy(
+            p_ref.at[pl.ds(NB * i, NB)], outs[k].at[:, pl.ds(NB * (c - k), NB)], out_sem.at[i])
+
+    def leave_last():
+        return pltpu.make_async_copy(p_ref.at[part(len(SUMMED) - 1, 0, 0)], outs[PANELS], out_sem.at[SUMMED[-1][0]])
 
     def stage(g, s):
-        order = [(scatter, 0), (scatter, 1), (scatter, 2), (gather, 2), (gather, 1), (gather, 0)]
+        order = steps_of(levels, g)
         if s > 0:
-            kind, depth = order[s - 1]
-            finish(kind, g, depth)
+            finish(*order[s - 1][:1], g, order[s - 1][1])
         if s < len(order):
-            kind, depth = order[s]
-            start(kind, g, depth)
+            start(order[s][0], g, order[s][1])
+        elif g == len(SUMMED) - 1:
+            leave_last().start()
         else:
             first, n = SUMMED[g]
             for i in range(first, first + n):
                 leave(i).start()
-
-    def leave(i):
-        rows = pl.ds(NB * i, NB) if i < OUTS - 1 else pl.ds(NB * i, p_ref.shape[0] - NB * i)
-        return pltpu.make_async_copy(p_ref.at[rows], outs[i], out_sem.at[i])
 
     def stages(p, first):
         for g, when in enumerate(WHEN):
@@ -482,14 +509,14 @@
         return carry
 
     lax.fori_loop(0, steps, step, 0)
-    leave(OUTS - 1).start()
-    for p in range(steps, max(WHEN[-1]) + 1):
+    for p in range(steps, max(w for when in WHEN for w in when) + 1):
         for g, when in enumerate(WHEN):
             for s, w in enumerate(when):
                 if w == p:
                     stage(g, s)
-    for i in range(OUTS):
+    for i in range(SUMMED[-1][0]):
         leave(i).wait()
+    leave_last().wait()
 
 
 def sweep(design_blk, target_col, tp_ways, dp_ways):
@@ -500,31 +527,33 @@
     steps = CHUNKS * PIECES
     peers = sum(level[1] - 1 for level in levels)
 
-    def landing(n):
-        rows, total = n * NB, 0
-        for level in levels:
-            rows //= level[1]
-            total += rows * (level[1] - 1)
+    def landing(g):
+        rows, total = SUMMED[g][1] * NB, 0
+        for back, depth in steps_of(levels, g):
+            if not back:
+                rows //= levels[depth][1]
+                total += rows * (levels[depth][1] - 1)
         return pltpu.VMEM((total, NB), F32)
 
     return pl.pallas_call(
-        functools.partial(sweep_kernel, levels),
-        out_shape=[jax.ShapeDtypeStruct((NB, NB), F32)] * (OUTS - 1) + [jax.ShapeDtypeStruct((CHUNKS * NB, NB), F32)],
+        functools.partial(sweep_kernel, levels, tp_ways),
+        out_shape=[jax.ShapeDtypeStruct((NB, NB * (LAST - k)), F32) for k in range(PANELS)]
+        + [jax.ShapeDtypeStruct((CHUNKS * NB // 2, NB), F32)],
         in_specs=[pl.BlockSpec(memory_space=pl.ANY), pl.BlockSpec(memory_space=pltpu.VMEM)],
-        out_specs=[pl.BlockSpec(memory_space=pl.ANY)] * OUTS,
+        out_specs=[pl.BlockSpec(memory_space=pl.ANY)] * (PANELS + 1),
         scratch_shapes=[
             pltpu.VMEM((blocks * NB, NB), F32),
             pltpu.VMEM((CHUNKS, tp_ways, sub_rows, NB // tp_ways), F32),
             pltpu.VMEM((3, piece, NB), BF16),
             pltpu.VMEM((1, NB), F32),
-            *(landing(n) for _, n in SUMMED),
+            *(landing(g) for g in range(len(SUMMED))),
             pltpu.SemaphoreType.DMA((steps, tp_ways - 1)),
             pltpu.SemaphoreType.DMA((steps, tp_ways - 1)),
             pltpu.SemaphoreType.DMA((CHUNKS,)),
             pltpu.SemaphoreType.DMA((len(SUMMED), 2, peers)),
             pltpu.SemaphoreType.DMA((len(SUMMED), 2, peers)),
             pltpu.SemaphoreType.REGULAR((len(SUMMED), len(levels))),
-            pltpu.SemaphoreType.DMA((OUTS,)),
+            pltpu.SemaphoreType.DMA((SUMMED[-1][0] + 1,)),
         ],
         compiler_params=pltpu.CompilerParams(collective_id=0, has_side_effects=True, vmem_limit_bytes=60 * 1024 * 1024),
         cost_estimate=pl.CostEstimate(flops=300_000_000_000, bytes_accessed=32_000_000, transcendentals=0),
@@ -555,12 +584,12 @@
     return out
 
 
-def sum_all(x, tp_ways, dp_ways):
+def sum_rest(x, tp_ways, dp_ways):
     tp, dp = lax.axis_index('tp'), lax.axis_index('dp')
     core = (dp & 1, 2, lambda v, m: swap(v, 'dp', dp_ways, m))
     plane = (dp >> 1, dp_ways // 2, lambda v, m: swap(v, 'dp', dp_ways, 2 * m))
     column = (tp, tp_ways, lambda v, m: swap(v, 'tp', tp_ways, m))
-    for level in (core, plane, column):
+    for level in (plane, column):
         x = scatter_sum(x, *level)
     for level in (column, plane, core):
         x = gather(x, *level)
@@ -576,23 +605,29 @@
         width = NB // tp_ways
         tp = lax.axis_index('tp')
         target_part = lax.dynamic_slice_in_dim(target_blk, tp * sub_rows, sub_rows)
-        *blocks, last = sweep(design_blk, target_part[:, None], tp_ways, dp_ways)
-        last = sum_all(last, tp_ways, dp_ways)
-        blocks += [last[NB * k:NB * (k + 1)] for k in range(CHUNKS)]
-
-        uppers, inverses, moments = {}, [], []
-        for c in range(CHUNKS):
-            total = blocks[c * (c + 1) // 2:]
-            moments.append(total[c][-2:, :NB // 2].reshape(1, NB))
-            for k in range(c + 1):
-                block = total[k]
-                for j in range(k):
-                    block = block - gram(uppers[j, k], uppers[j, c])
-                if k < c:
-                    uppers[k, c] = jnp.dot(inverses[k], block, precision=HIGHEST, preferred_element_type=F32)
-                else:
-                    inverses.append(diag_inverse(block, ridge))
-        order, residual = finish(jnp.concatenate(moments, axis=0), target_blk, design_blk, uppers, inverses, tp_ways)
+        *panels, last = sweep(design_blk, target_part[:, None], tp_ways, dp_ways)
+        last = sum_rest(last, tp_ways, dp_ways)
+        moments = [panel[NB - 2:, :NB // 2] for panel in panels] + [last[-2:, :NB // 2]]
+
+        uppers, tops, inverses = [], [], []
+        for k in range(PANELS):
+            inverses.append(diag_inverse(panels[k], ridge))
+            if k < PANELS - 1:
+                upper = jnp.dot(inverses[k], panels[k][:, NB:], precision=HIGHEST, preferred_element_type=F32)
+                uppers.append(upper)
+                for r in range(k + 1, PANELS):
+                    at = NB * (r - k - 1)
+                    panels[r] = panels[r] - gram(upper[:, at:at + NB], upper[:, at:])
+        corner = last[NB * LAST:]
+        rest = last[:NB * LAST]
+        for k in range(PANELS):
+            tops.append(jnp.dot(inverses[k], rest[:NB], precision=HIGHEST, preferred_element_type=F32))
+            if k < PANELS - 1:
+                rest = rest[NB:] - gram(uppers[k], tops[k])
+            corner = corner - gram(tops[k], tops[k])
+        inverses.append(diag_inverse(corner, ridge))
+        moment = jnp.concatenate([m.reshape(1, NB) for m in moments], axis=0)
+        order, residual = finish(moment, target_blk, design_blk, uppers, tops, inverses, tp_ways)
         coeffs = order.reshape(CHUNKS, tp_ways, width).transpose(1, 0, 2).reshape(-1)
         return coeffs, residual.reshape(-1)
 

time: 749 us -> 703 us (0.939)
  waiting for transfers between devices: 51.9 us -> 31.5 us
  Pallas kernels: 561 us -> 545 us
    ppermute x14 -> x13, waiting for transfers between devices: 51.9 us -> 31.5 us  [swap(): return lax.ppermute(x, axis, [(i, i ^ mask) for i in range(ways)])]
    pallas_call x1, Pallas kernels: 440 us -> 429 us  [sweep(): pl.pallas_call(functools.partial(sweep_kernel, levels, tp_ways), out_shap...]
    dot_general x20 -> x13, matrix products: 50.8 us -> 46.7 us  [gram(): lax.dot_general(left, right, CONTRACT_ROWS, precision=HIGHEST, preferred_...]
    dot_general x10 -> x7, matrix products: 24.7 us -> 23.8 us  [the longest x3 16.1 us: local_fit(): jnp.dot(inverses[k], panels[k][:, NB:], precision=HIGHEST, preferred_elem...]
    ppermute x14 -> x13, starting transfers between devices: 16.6 us -> 15.8 us  [swap(): return lax.ppermute(x, axis, [(i, i ^ mask) for i in range(ways)])]
  transfers between devices with their start and end apart: 14 -> 13, of which waited for: 7 -> 7; matrix products, arithmetic and copies ran while one was open for 8% -> 8% of each run, Pallas kernels for 11% -> 11%
where the time goes in v1:
time: 703 us; the launch traced here: 696 us
  Pallas kernels  545 us (78%)
  matrix products  70.5 us (10%)
  waiting for transfers between devices  31.5 us (4%)
  local copies, waits for them, and re-layouts  28 us (4%)
  starting transfers between devices  15.8 us (2%)
    pallas_call x1, Pallas kernels, sweep(): pl.pallas_call(functools.partial(sweep_kernel, levels, tp_ways), out_shap...  429 us
    pallas_call x5, Pallas kernels, diag_inverse(): pl.pallas_call(diag_kernel, out_shape=jax.ShapeDtypeStruct((n, n), F32),...  98.3 us
    dot_general x13, matrix products, gram(): lax.dot_general(left, right, CONTRACT_ROWS, precision=HIGHEST, preferred_...  46.7 us
    ppermute x13, waiting for transfers between devices, swap(): return lax.ppermute(x, axis, [(i, i ^ mask) for i in range(ways)])  31.5 us
    pallas_call x1, Pallas kernels, finish(): pl.pallas_call(functools.partial(finish_kernel, ways), out_shape=(jax.Sha...  18 us
    dot_general x3, matrix products, local_fit(): jnp.dot(inverses[k], panels[k][:, NB:], precision=HIGHEST, preferred_elem...  16.1 us
    ppermute x13, starting transfers between devices, swap(): return lax.ppermute(x, axis, [(i, i ^ mask) for i in range(ways)])  15.8 us
  transfers between devices with their start and end apart: 13, of which 7 were waited for; matrix products, arithmetic and copies ran while one was open for 8% of the time, Pallas kernels for 11%

profile of v1, /device:TPU:0, one launch (start us, length us, event | category | flops | bytes accessed | tf_op | source)
XLA Modules:
  0.0 696.0 jit_solution(6068325442127782390)
XLA Ops:
  2.6 429.1 %sweep.1 = (f32[512,2048]{1,0:T(8,128)}, f32[512,1536]{1,0:T(8,128)}, f32[512,1024]{1,0:T(8,128)}, f32[512,512]{1,0:T(8,128)}, f32[1280,512]{1,0:T(8,128)}) custom-call(f32[6144,640]{1,0:T(8,128)} %a_hbm.1, f32[1536,1]{1,0:T(8,128)} %broadcast_in_dim.16.b_ref), custom_call_target="tpu_custom_call" | custom-call | flops 299999985664 | bytes 32000000 | tf_op jit(solution)/shard_map/sweep/pallas_call | solution.py:538
  438.7 19.6 %diag_inverse.5.refs_7_ = f32[512,512]{1,0:T(8,128)} custom-call(f32[1]{0:T(128)} %bitcast.78.lam_ref, f32[512,2048]{1,0:T(8,128)} %get-tuple-element.9.s_ref), custom_call_target="tpu_custom_call" | custom-call | flops 20000000000 | bytes 2097152 | tf_op jit(solution)/shard_map/diag_inverse/pallas_call | solution.py:159
  458.3 7.5 %fusion.refs_0_ = f32[512,1536]{1,0:T(8,128)S(1)} fusion(f32[512,512]{1,0:T(8,128)} %diag_inverse.5.refs_7_, f32[512,2048]{1,0:T(8,128)} %get-tuple-element.9.s_ref), kind=kOutput, calls=%fused_computation.2 | convolution fusion | flops 4831838208 | bytes 7340032 | tf_op jit(solution)/shard_map/dot_general | solution.py:616
  465.9 7.1 %convolution_subtract_fusion.s_ref = f32[512,1536]{1,0:T(8,128)} fusion(f32[512,1536]{1,0:T(8,128)S(1)} %copy-done.16, f32[512,1536]{1,0:T(8,128)S(1)} %fusion.refs_0_), kind=kOutput, calls=%fused_computation | convolution fusion | flops 4832624640 | bytes 10485760 | tf_op jit(solution)/shard_map/dot_general | solution.py:275
  473.0 19.8 %diag_inverse.6.refs_8_ = f32[512,512]{1,0:T(8,128)} custom-call(f32[1]{0:T(128)} %bitcast.79.lam_ref, f32[512,1536]{1,0:T(8,128)} %convolution_subtract_fusion.s_ref), custom_call_target="tpu_custom_call" | custom-call | flops 20000000000 | bytes 2097152 | tf_op jit(solution)/shard_map/diag_inverse/pallas_call | solution.py:159
  492.8 5.5 fusion.4.refs_1_
  499.6 3.6 fusion.22
  503.2 5.0 subtract_subtract_fusion.s_ref
  508.3 19.6 %diag_inverse.7.refs_9_ = f32[512,512]{1,0:T(8,128)} custom-call(f32[1]{0:T(128)} %bitcast.80.lam_ref, f32[512,1024]{1,0:T(8,128)} %subtract_subtract_fusion.s_ref), custom_call_target="tpu_custom_call" | custom-call | flops 20000000000 | bytes 2097152 | tf_op jit(solution)/shard_map/diag_inverse/pallas_call | solution.py:159
  534.4 3.1 fusion.20.refs_2_
  539.0 8.8 %collective-permute-done.4 = f32[80,512]{1,0:T(8,128)S(1)} collective-permute-done((f32[80,512]{1,0:T(8,128)S(1)}, f32[80,512]{1,0:T(8,128)S(1)}, u32[]{:S(2)}, u32[]{:S(2)}) %collective-permute-start.4) | collective-permute-done | bytes 163872 | tf_op jit(solution)/shard_map/ppermute | solution.py:565
  549.5 3.2 collective-permute-start.7
  552.7 4.5 convolution_subtract_fusion.3
  561.4 3.3 collective-permute-done.8
  569.5 4.1 convolution_subtract_fusion.2
  577.6 5.6 collective-permute-done.9
  585.3 10.6 %collective-permute-done.10 = f32[320,512]{1,0:T(8,128)} collective-permute-done((f32[320,512]{1,0:T(8,128)}, f32[320,512]{1,0:T(8,128)}, u32[]{:S(2)}, u32[]{:S(2)}) %collective-permute-start.10) | collective-permute-done | bytes 655392 | tf_op jit(solution)/shard_map/ppermute | solution.py:565
  599.5 2.9 convolution_subtract_fusion.1.s_ref
  602.4 19.8 %diag_inverse.8.refs_10_ = f32[512,512]{1,0:T(8,128)} custom-call(f32[1]{0:T(128)} %bitcast.81.lam_ref, f32[512,512]{1,0:T(8,128)} %convolution_subtract_fusion.1.s_ref), custom_call_target="tpu_custom_call" | custom-call | flops 20000000000 | bytes 2097152 | tf_op jit(solution)/shard_map/diag_inverse/pallas_call | solution.py:159
  629.0 5.2 slice_subtract_fusion
  636.1 3.8 slice_subtract_fusion.1
  651.4 3.2 fusion.10.s_ref
  654.7 19.4 %diag_inverse.9.refs_11_ = f32[512,512]{1,0:T(8,128)} custom-call(f32[1]{0:T(128)} %bitcast.82.lam_ref, f32[512,512]{1,0:T(8,128)} %fusion.10.s_ref), custom_call_target="tpu_custom_call" | custom-call | flops 20000000000 | bytes 2097152 | tf_op jit(solution)/shard_map/diag_inverse/pallas_call | solution.py:159
  676.6 18.0 %finish.1 = (f32[5,512]{1,0:T(8,128)S(1)}, f32[48,128]{1,0:T(8,128)S(1)}) custom-call(f32[5,512]{1,0:T(8,128)S(1)} %concatenate.3.h_ref, f32[48,128]{1,0:T(8,128)S(1)} %bitcast.83, f32[6144,640]{1,0:T(8,128)} %a_hbm.1, f32[512,1536]{1,0:T(8,128)} %copy-done.5, f32[512,1024]{1,0:T(8,128)} %copy-done.7, f32[512,512]{1,0:T(8,128)S(1)} %fusion.20.refs_2_, ...), custom_call_target="tpu_custom_call" | custom-call | flops 5000000000 | bytes 32000000 | tf_op jit(solution)/shard_map/finish/pallas_call | solution.py:250
  (96 shorter events, 61.7 us)
Async XLA Ops:
  434.6 93.3 %collective-permute-start.2 = (f32[320,512]{1,0:T(8,128)}, f32[320,512]{1,0:T(8,128)}, u32[]{:S(2)}, u32[]{:S(2)}) collective-permute-start(f32[320,512]{1,0:T(8,128)} %get-tuple-element.19), channel_id=1, source_target_pairs={{0,6},{1,7},{2,4},{3,5},{4,2},{5,3},{6,0},{7,1},{8,14},{9,15},{10,... | collective-permute-start | bytes 1966088 | tf_op jit(solution)/shard_map/ppermute | solution.py:565
  436.0 91.9 %collective-permute-start.1 = (f32[320,512]{1,0:T(8,128)}, f32[320,512]{1,0:T(8,128)}, u32[]{:S(2)}, u32[]{:S(2)}) collective-permute-start(f32[320,512]{1,0:T(8,128)} %get-tuple-element.20), channel_id=1, source_target_pairs={{0,4},{1,5},{2,6},{3,7},{4,0},{5,1},{6,2},{7,3},{8,12},{9,13},{10,... | collective-permute-start | bytes 1966088 | tf_op jit(solution)/shard_map/ppermute | solution.py:565
  437.5 90.4 %collective-permute-start = (f32[320,512]{1,0:T(8,128)}, f32[320,512]{1,0:T(8,128)}, u32[]{:S(2)}, u32[]{:S(2)}) collective-permute-start(f32[320,512]{1,0:T(8,128)} %get-tuple-element.18), channel_id=1, source_target_pairs={{0,2},{1,3},{2,0},{3,1},{4,6},{5,7},{6,4},{7,5},{8,10},{9,11},{10,... | collective-permute-start | bytes 1966088 | tf_op jit(solution)/shard_map/ppermute | solution.py:565
  458.3 7.6 %copy-start.16 = (f32[512,1536]{1,0:T(8,128)S(1)}, f32[512,1536]{1,0:T(8,128)}, u32[]{:S(2)}) copy-start(f32[512,1536]{1,0:T(8,128)} %get-tuple-element.10) | copy-start | bytes 9437188
  465.9 37.4 %copy-start.5 = (f32[512,1536]{1,0:T(8,128)}, f32[512,1536]{1,0:T(8,128)S(1)}, u32[]{:S(2)}) copy-start(f32[512,1536]{1,0:T(8,128)S(1)} %fusion.refs_0_) | copy-start | bytes 9437188
  527.9 6.6 copy-start.12
  530.0 22.7 %copy-start.18 = (f32[512,512]{1,0:T(8,128)S(1)}, f32[512,512]{1,0:T(8,128)}, u32[]{:S(2)}) copy-start(f32[512,512]{1,0:T(8,128)} %get-tuple-element.12) | copy-start | bytes 3145732
  530.0 9.0 %collective-permute-start.5 = (f32[80,512]{1,0:T(8,128)S(1)}, f32[80,512]{1,0:T(8,128)S(1)}, u32[]{:S(2)}, u32[]{:S(2)}) collective-permute-start(f32[80,512]{1,0:T(8,128)S(1)} %get-tuple-element.22), channel_id=1, source_target_pairs={{0,24},{8,16},{16,8},{24,0},{1,25},{9,17},{17,9},{25,1},{2,26},{10... | collective-permute-start | bytes 491528 | tf_op jit(solution)/shard_map/ppermute | solution.py:565
  532.7 15.2 %collective-permute-start.4 = (f32[80,512]{1,0:T(8,128)S(1)}, f32[80,512]{1,0:T(8,128)S(1)}, u32[]{:S(2)}, u32[]{:S(2)}) collective-permute-start(f32[80,512]{1,0:T(8,128)S(1)} %get-tuple-element.23), channel_id=1, source_target_pairs={{0,16},{8,24},{16,0},{24,8},{1,17},{9,25},{17,1},{25,9},{2,18},{10... | collective-permute-start | bytes 491528 | tf_op jit(solution)/shard_map/ppermute | solution.py:565
  533.5 14.4 %collective-permute-start.3 = (f32[80,512]{1,0:T(8,128)S(1)}, f32[80,512]{1,0:T(8,128)S(1)}, u32[]{:S(2)}, u32[]{:S(2)}) collective-permute-start(f32[80,512]{1,0:T(8,128)S(1)} %get-tuple-element.21), channel_id=1, source_target_pairs={{0,8},{8,0},{16,24},{24,16},{1,9},{9,1},{17,25},{25,17},{2,10},{10... | collective-permute-start | bytes 491528 | tf_op jit(solution)/shard_map/ppermute | solution.py:565
  548.7 20.8 %copy-start.8 = (f32[512,1024]{1,0:T(8,128)S(1)}, f32[512,1024]{1,0:T(8,128)}, u32[]{:S(2)}) copy-start(f32[512,1024]{1,0:T(8,128)} %copy-done.7) | copy-start | bytes 6291460
  549.5 9.4 %collective-permute-start.6 = (f32[80,512]{1,0:T(8,128)}, f32[80,512]{1,0:T(8,128)S(1)}, u32[]{:S(2)}, u32[]{:S(2)}) collective-permute-start(f32[80,512]{1,0:T(8,128)} %get-tuple-element.17), channel_id=1, source_target_pairs={{0,8},{8,0},{16,24},{24,16},{1,9},{9,1},{17,25},{25,17},{2,10},{10... | collective-permute-start | bytes 491528 | tf_op jit(solution)/shard_map/ppermute | solution.py:565
  549.5 11.2 %collective-permute-start.7 = (f32[80,512]{1,0:T(8,128)}, f32[80,512]{1,0:T(8,128)S(1)}, u32[]{:S(2)}, u32[]{:S(2)}) collective-permute-start(f32[80,512]{1,0:T(8,128)} %get-tuple-element.17), channel_id=1, source_target_pairs={{0,16},{8,24},{16,0},{24,8},{1,17},{9,25},{17,1},{25,9},{2,18},{10... | collective-permute-start | bytes 491528 | tf_op jit(solution)/shard_map/ppermute | solution.py:565
  557.2 7.5 %collective-permute-start.8 = (f32[80,512]{1,0:T(8,128)}, f32[80,512]{1,0:T(8,128)S(1)}, u32[]{:S(2)}, u32[]{:S(2)}) collective-permute-start(f32[80,512]{1,0:T(8,128)} %get-tuple-element.17), channel_id=1, source_target_pairs={{0,24},{8,16},{16,8},{24,0},{1,25},{9,17},{17,9},{25,1},{2,26},{10... | collective-permute-start | bytes 491528 | tf_op jit(solution)/shard_map/ppermute | solution.py:565
  565.3 17.9 %collective-permute-start.9 = (f32[320,512]{1,0:T(8,128)}, f32[320,512]{1,0:T(8,128)}, u32[]{:S(2)}, u32[]{:S(2)}) collective-permute-start(f32[320,512]{1,0:T(8,128)} %constant_dynamic-update-slice_fusion.6), channel_id=1, source_target_pairs={{0,2},{1,3},{2,0},{3,1},{4,6},{5,7},{6,4},{7,5},{8,10},{9,11},{10,... | collective-permute-start | bytes 1966088 | tf_op jit(solution)/shard_map/ppermute | solution.py:565
  566.8 29.1 %collective-permute-start.10 = (f32[320,512]{1,0:T(8,128)}, f32[320,512]{1,0:T(8,128)}, u32[]{:S(2)}, u32[]{:S(2)}) collective-permute-start(f32[320,512]{1,0:T(8,128)} %constant_dynamic-update-slice_fusion.6), channel_id=1, source_target_pairs={{0,4},{1,5},{2,6},{3,7},{4,0},{5,1},{6,2},{7,3},{8,12},{9,13},{10,... | collective-permute-start | bytes 1966088 | tf_op jit(solution)/shard_map/ppermute | solution.py:565
  568.0 29.9 %collective-permute-start.11 = (f32[320,512]{1,0:T(8,128)}, f32[320,512]{1,0:T(8,128)S(1)}, u32[]{:S(2)}, u32[]{:S(2)}) collective-permute-start(f32[320,512]{1,0:T(8,128)} %constant_dynamic-update-slice_fusion.6), channel_id=1, source_target_pairs={{0,6},{1,7},{2,4},{3,5},{4,2},{5,3},{6,0},{7,1},{8,14},{9,15},{10,... | collective-permute-start | bytes 1966088 | tf_op jit(solution)/shard_map/ppermute | solution.py:565
  575.5 24.0 %copy-start.14 = (f32[512,512]{1,0:T(8,128)S(1)}, f32[512,512]{1,0:T(8,128)}, u32[]{:S(2)}) copy-start(f32[512,512]{1,0:T(8,128)} %convolution_subtract_fusion.2) | copy-start | bytes 3145732
  598.8 26.2 %collective-permute-start.12 = (f32[1280,512]{1,0:T(8,128)}, f32[1280,512]{1,0:T(8,128)}, u32[]{:S(2)}, u32[]{:S(2)}) collective-permute-start(f32[1280,512]{1,0:T(8,128)} %constant_dynamic-update-slice_fusion.2), channel_id=1, source_target_pairs={{0,1},{1,0},{2,3},{3,2},{4,5},{5,4},{6,7},{7,6},{8,9},{9,8},{10,11... | collective-permute-start | bytes 7864328 | tf_op jit(solution)/shard_map/ppermute | solution.py:565
  629.0 5.2 copy-start.11
  636.1 3.8 copy-start.13
  641.8 3.7 copy-start
  645.5 3.8 copy-start.15
  654.7 19.4 %copy-start.4 = (f32[6144]{0:T(1024)S(1)}, f32[6144]{0:T(1024)}, u32[]{:S(2)}) copy-start(f32[6144]{0:T(1024)} %param.4) | copy-start | bytes 73732
  (8 other events, 16.6 us)

commit v2 on v1

--- a/solution.py
+++ b/solution.py
@@ -281,9 +281,9 @@
 PANELS = LAST
 SUMMED = ((0, 3), (3, 3), (6, 4), (10, 5))
 WHEN = (
-    (11, 12, 14, 16, 18, 20, 22, 24, 25),
-    (17, 18, 20, 22, 24, 26, 28, 30, 31),
-    (23, 24, 26, 28, 30, 31, 32, 33, 34),
+    (11, 12, 14, 15, 16, 17, 18, 20, 21),
+    (17, 18, 21, 22, 23, 24, 26, 28, 29),
+    (23, 24, 26, 27, 28, 29, 30, 31, 32),
     (29, 30),
 )
 
@@ -457,6 +457,8 @@
         for m in range(1, ways):
             travel(p, m).wait()
 
+        stages(p, False)
+
         @pl.when(p + AHEAD < steps)
         def _():
             for m in range(1, ways):
@@ -467,7 +469,6 @@
             own(c).wait()
             moment[...] = jnp.zeros_like(moment)
 
-        stages(p, False)
         new = load(c, r)
         for i, x in enumerate(split3(new)):
             right[i] = x
@@ -578,10 +579,14 @@
 
 
 def gather(x, me, ways, send):
-    out = jnp.zeros((ways * x.shape[0], x.shape[1]), x.dtype)
-    for m in range(ways):
-        out = lax.dynamic_update_slice(out, send(x, m) if m else x, ((me ^ m) * x.shape[0], 0))
-    return out
+    got = [x] + [send(x, m) for m in range(1, ways)]
+    rows = []
+    for i in range(ways):
+        part = got[ways - 1]
+        for m in range(ways - 1):
+            part = jnp.where(me == i ^ m, got[m], part)
+        rows.append(part)
+    return jnp.concatenate(rows, axis=0)
 
 
 def sum_rest(x, tp_ways, dp_ways):
@@ -616,8 +621,10 @@
                 upper = jnp.dot(inverses[k], panels[k][:, NB:], precision=HIGHEST, preferred_element_type=F32)
                 uppers.append(upper)
                 for r in range(k + 1, PANELS):
-                    at = NB * (r - k - 1)
-                    panels[r] = panels[r] - gram(upper[:, at:at + NB], upper[:, at:])
+                    right = upper[:, NB * (r - k - 1):]
+                    if r == PANELS - 1:
+                        right = lax.optimization_barrier(right)
+                    panels[r] = panels[r] - gram(right[:, :NB], right)
         corner = last[NB * LAST:]
         rest = last[:NB * LAST]
         for k in range(PANELS):

time: 703 us -> 676 us (0.962)
  Pallas kernels: 545 us -> 527 us
  local copies, waits for them, and re-layouts: 28 us -> 15.4 us
  other arithmetic: 2.85 us -> 13.5 us
    pallas_call x1, Pallas kernels: 429 us -> 412 us  [sweep(): pl.pallas_call(functools.partial(sweep_kernel, levels, tp_ways), out_shap...]
    dynamic_update_slice x9 -> x0, local copies, waits for them, and re-layouts: 13.2 us -> none  [gather(): lax.dynamic_update_slice(out, send(x, m) if m else x, ((me ^ m) * x.shape...]
    select_n x0 -> x4, other arithmetic: none -> 7.59 us  [gather(): part = jnp.where(me == i ^ m, got[m], part)]
  transfers between devices with their start and end apart: 13 -> 13, of which waited for: 7 -> 4; matrix products, arithmetic and copies ran while one was open for 8% -> 6% of each run, Pallas kernels for 11% -> 12%
where the time goes in v2:
time: 676 us; the launch traced here: 669 us
  Pallas kernels  527 us (78%)
  matrix products  68.9 us (10%)
  waiting for transfers between devices  26.2 us (4%)
  starting transfers between devices  15.8 us (2%)
  local copies, waits for them, and re-layouts  15.4 us (2%)
  other arithmetic  13.5 us (2%)
    pallas_call x1, Pallas kernels, sweep(): pl.pallas_call(functools.partial(sweep_kernel, levels, tp_ways), out_shap...  412 us
    pallas_call x5, Pallas kernels, diag_inverse(): pl.pallas_call(diag_kernel, out_shape=jax.ShapeDtypeStruct((n, n), F32),...  98.3 us
    dot_general x13, matrix products, gram(): lax.dot_general(left, right, CONTRACT_ROWS, precision=HIGHEST, preferred_...  45.2 us
    ppermute x13, waiting for transfers between devices, swap(): return lax.ppermute(x, axis, [(i, i ^ mask) for i in range(ways)])  26.2 us
    pallas_call x1, Pallas kernels, finish(): pl.pallas_call(functools.partial(finish_kernel, ways), out_shape=(jax.Sha...  16.2 us
    dot_general x3, matrix products, local_fit(): jnp.dot(inverses[k], panels[k][:, NB:], precision=HIGHEST, preferred_elem...  16 us
    ppermute x13, starting transfers between devices, swap(): return lax.ppermute(x, axis, [(i, i ^ mask) for i in range(ways)])  15.8 us
  transfers between devices with their start and end apart: 13, of which 4 were waited for; matrix products, arithmetic and copies ran while one was open for 6% of the time, Pallas kernels for 12%

profile of v2, /device:TPU:0, one launch (start us, length us, event | category | flops | bytes accessed | tf_op | source)
XLA Modules:
  0.0 669.0 jit_solution(1167759791048167387)
XLA Ops:
  2.6 412.4 %sweep.1 = (f32[512,2048]{1,0:T(8,128)}, f32[512,1536]{1,0:T(8,128)}, f32[512,1024]{1,0:T(8,128)}, f32[512,512]{1,0:T(8,128)}, f32[1280,512]{1,0:T(8,128)}) custom-call(f32[6144,640]{1,0:T(8,128)} %a_hbm.1, f32[1536,1]{1,0:T(8,128)} %broadcast_in_dim.4.b_ref), custom_call_target="tpu_custom_call" | custom-call | flops 299999985664 | bytes 32000000 | tf_op jit(solution)/shard_map/sweep/pallas_call | solution.py:539
  415.0 2.9 dynamic-slice_bitcast_fusion.2
  422.0 19.6 %diag_inverse.5.refs_7_ = f32[512,512]{1,0:T(8,128)} custom-call(f32[1]{0:T(128)} %bitcast.81.lam_ref, f32[512,2048]{1,0:T(8,128)} %get-tuple-element.9.s_ref), custom_call_target="tpu_custom_call" | custom-call | flops 20000000000 | bytes 2097152 | tf_op jit(solution)/shard_map/diag_inverse/pallas_call | solution.py:159
  441.6 7.4 %fusion.1.refs_0_ = f32[512,1536]{1,0:T(8,128)S(1)} fusion(f32[512,512]{1,0:T(8,128)} %diag_inverse.5.refs_7_, f32[512,2048]{1,0:T(8,128)} %get-tuple-element.9.s_ref), kind=kOutput, calls=%fused_computation.3 | convolution fusion | flops 4831838208 | bytes 7340032 | tf_op jit(solution)/shard_map/dot_general | solution.py:621
  449.1 9.4 %convolution_subtract_fusion.s_ref = f32[512,1536]{1,0:T(8,128)} fusion(f32[512,1536]{1,0:T(8,128)} %get-tuple-element.10, f32[512,1536]{1,0:T(8,128)S(1)} %fusion.1.refs_0_), kind=kOutput, calls=%fused_computation | convolution fusion | flops 4832624640 | bytes 10485760 | tf_op jit(solution)/shard_map/dot_general | solution.py:275
  458.5 19.8 %diag_inverse.6.refs_8_ = f32[512,512]{1,0:T(8,128)} custom-call(f32[1]{0:T(128)} %bitcast.82.lam_ref, f32[512,1536]{1,0:T(8,128)} %convolution_subtract_fusion.s_ref), custom_call_target="tpu_custom_call" | custom-call | flops 20000000000 | bytes 2097152 | tf_op jit(solution)/shard_map/diag_inverse/pallas_call | solution.py:159
  478.3 5.5 fusion.5.refs_1_
  483.8 3.6 fusion.21
  491.2 3.0 collective-permute-start.5
  495.6 5.0 subtract_subtract_fusion.s_ref
  500.6 7.6 %collective-permute-done.4 = f32[80,512]{1,0:T(8,128)} collective-permute-done((f32[80,512]{1,0:T(8,128)}, f32[80,512]{1,0:T(8,128)}, u32[]{:S(2)}, u32[]{:S(2)}) %collective-permute-start.4) | collective-permute-done | bytes 163872 | tf_op jit(solution)/shard_map/ppermute | solution.py:566
  509.4 3.2 collective-permute-start.7
  513.8 19.6 %diag_inverse.7.refs_9_ = f32[512,512]{1,0:T(8,128)} custom-call(f32[1]{0:T(128)} %bitcast.83.lam_ref, f32[512,1024]{1,0:T(8,128)} %subtract_subtract_fusion.s_ref), custom_call_target="tpu_custom_call" | custom-call | flops 20000000000 | bytes 2097152 | tf_op jit(solution)/shard_map/diag_inverse/pallas_call | solution.py:159
  542.3 3.1 fusion.19.refs_2_
  545.5 2.8 convolution_subtract_fusion.3
  548.4 5.5 collective-permute-done.9
  555.4 11.6 %collective-permute-done.11 = f32[320,512]{1,0:T(8,128)} collective-permute-done((f32[320,512]{1,0:T(8,128)}, f32[320,512]{1,0:T(8,128)}, u32[]{:S(2)}, u32[]{:S(2)}) %collective-permute-start.11) | collective-permute-done | bytes 655392 | tf_op jit(solution)/shard_map/ppermute | solution.py:566
  576.3 2.8 convolution_subtract_fusion.1.s_ref
  579.2 19.9 %diag_inverse.8.refs_10_ = f32[512,512]{1,0:T(8,128)} custom-call(f32[1]{0:T(128)} %bitcast.84.lam_ref, f32[512,512]{1,0:T(8,128)} %convolution_subtract_fusion.1.s_ref), custom_call_target="tpu_custom_call" | custom-call | flops 20000000000 | bytes 2097152 | tf_op jit(solution)/shard_map/diag_inverse/pallas_call | solution.py:159
  603.7 5.3 fusion
  611.0 3.8 slice_subtract_fusion
  626.3 3.1 fusion.11.s_ref
  629.4 19.4 %diag_inverse.9.refs_11_ = f32[512,512]{1,0:T(8,128)} custom-call(f32[1]{0:T(128)} %bitcast.85.lam_ref, f32[512,512]{1,0:T(8,128)} %fusion.11.s_ref), custom_call_target="tpu_custom_call" | custom-call | flops 20000000000 | bytes 2097152 | tf_op jit(solution)/shard_map/diag_inverse/pallas_call | solution.py:159
  651.3 16.2 %finish.1 = (f32[5,512]{1,0:T(8,128)S(1)}, f32[48,128]{1,0:T(8,128)S(1)}) custom-call(f32[5,512]{1,0:T(8,128)S(1)} %concatenate.14.h_ref, f32[48,128]{1,0:T(8,128)S(1)} %bitcast.86, f32[6144,640]{1,0:T(8,128)} %a_hbm.1, f32[512,1536]{1,0:T(8,128)} %copy-done.5, f32[512,1024]{1,0:T(8,128)} %copy-done.7, f32[512,512]{1,0:T(8,128)S(1)} %fusion.19.refs_2_, ...), custom_call_target="tpu_custom_call" | custom-call | flops 5000000000 | bytes 32000000 | tf_op jit(solution)/shard_map/finish/pallas_call | solution.py:250
  (114 shorter events, 54.2 us)
Async XLA Ops:
  417.9 69.6 %collective-permute-start.2 = (f32[320,512]{1,0:T(8,128)}, f32[320,512]{1,0:T(8,128)}, u32[]{:S(2)}, u32[]{:S(2)}) collective-permute-start(f32[320,512]{1,0:T(8,128)} %get-tuple-element.22), channel_id=1, source_target_pairs={{0,6},{1,7},{2,4},{3,5},{4,2},{5,3},{6,0},{7,1},{8,14},{9,15},{10,... | collective-permute-start | bytes 1966088 | tf_op jit(solution)/shard_map/ppermute | solution.py:566
  419.6 67.8 %collective-permute-start.1 = (f32[320,512]{1,0:T(8,128)}, f32[320,512]{1,0:T(8,128)}, u32[]{:S(2)}, u32[]{:S(2)}) collective-permute-start(f32[320,512]{1,0:T(8,128)} %get-tuple-element.23), channel_id=1, source_target_pairs={{0,4},{1,5},{2,6},{3,7},{4,0},{5,1},{6,2},{7,3},{8,12},{9,13},{10,... | collective-permute-start | bytes 1966088 | tf_op jit(solution)/shard_map/ppermute | solution.py:566
  419.9 67.6 %collective-permute-start = (f32[320,512]{1,0:T(8,128)}, f32[320,512]{1,0:T(8,128)}, u32[]{:S(2)}, u32[]{:S(2)}) collective-permute-start(f32[320,512]{1,0:T(8,128)} %get-tuple-element.21), channel_id=1, source_target_pairs={{0,2},{1,3},{2,0},{3,1},{4,6},{5,7},{6,4},{7,5},{8,10},{9,11},{10,... | collective-permute-start | bytes 1966088 | tf_op jit(solution)/shard_map/ppermute | solution.py:566
  449.0 92.1 %copy-start.5 = (f32[512,1536]{1,0:T(8,128)}, f32[512,1536]{1,0:T(8,128)S(1)}, u32[]{:S(2)}) copy-start(f32[512,1536]{1,0:T(8,128)S(1)} %fusion.1.refs_0_) | copy-start | bytes 9437188
  483.8 5.8 copy-start.7
  487.4 8.2 %copy-start.25 = (f32[512,1024]{1,0:T(8,128)S(1)}, f32[512,1024]{1,0:T(8,128)}, u32[]{:S(2)}) copy-start(f32[512,1024]{1,0:T(8,128)} %get-tuple-element.11) | copy-start | bytes 6291460
  491.2 9.4 %collective-permute-start.5 = (f32[80,512]{1,0:T(8,128)}, f32[80,512]{1,0:T(8,128)S(1)}, u32[]{:S(2)}, u32[]{:S(2)}) collective-permute-start(f32[80,512]{1,0:T(8,128)} %get-tuple-element.29), channel_id=1, source_target_pairs={{0,24},{8,16},{16,8},{24,0},{1,25},{9,17},{17,9},{25,1},{2,26},{10... | collective-permute-start | bytes 491528 | tf_op jit(solution)/shard_map/ppermute | solution.py:566
  494.3 14.0 %collective-permute-start.4 = (f32[80,512]{1,0:T(8,128)}, f32[80,512]{1,0:T(8,128)}, u32[]{:S(2)}, u32[]{:S(2)}) collective-permute-start(f32[80,512]{1,0:T(8,128)} %get-tuple-element.30), channel_id=1, source_target_pairs={{0,16},{8,24},{16,0},{24,8},{1,17},{9,25},{17,1},{25,9},{2,18},{10... | collective-permute-start | bytes 491528 | tf_op jit(solution)/shard_map/ppermute | solution.py:566
  494.3 14.0 %collective-permute-start.3 = (f32[80,512]{1,0:T(8,128)S(1)}, f32[80,512]{1,0:T(8,128)}, u32[]{:S(2)}, u32[]{:S(2)}) collective-permute-start(f32[80,512]{1,0:T(8,128)S(1)} %get-tuple-element.28), channel_id=1, source_target_pairs={{0,8},{8,0},{16,24},{24,16},{1,9},{9,1},{17,25},{25,17},{2,10},{10... | collective-permute-start | bytes 491528 | tf_op jit(solution)/shard_map/ppermute | solution.py:566
  509.3 24.1 %copy-start.27 = (f32[80,512]{1,0:T(8,128)}, f32[80,512]{1,0:T(8,128)S(1)}, u32[]{:S(2)}) copy-start(f32[80,512]{1,0:T(8,128)S(1)} %fusion.28) | copy-start | bytes 491524
  509.3 24.1 %collective-permute-start.6 = (f32[80,512]{1,0:T(8,128)S(1)}, f32[80,512]{1,0:T(8,128)S(1)}, u32[]{:S(2)}, u32[]{:S(2)}) collective-permute-start(f32[80,512]{1,0:T(8,128)S(1)} %fusion.28), channel_id=1, source_target_pairs={{0,16},{8,24},{16,0},{24,8},{1,17},{9,25},{17,1},{25,9},{2,18},{10... | collective-permute-start | bytes 491528 | tf_op jit(solution)/shard_map/ppermute | solution.py:566
  509.4 24.0 %collective-permute-start.7 = (f32[80,512]{1,0:T(8,128)S(1)}, f32[80,512]{1,0:T(8,128)}, u32[]{:S(2)}, u32[]{:S(2)}) collective-permute-start(f32[80,512]{1,0:T(8,128)S(1)} %fusion.28), channel_id=1, source_target_pairs={{0,8},{8,0},{16,24},{24,16},{1,9},{9,1},{17,25},{25,17},{2,10},{10... | collective-permute-start | bytes 491528 | tf_op jit(solution)/shard_map/ppermute | solution.py:566
  512.6 21.5 %collective-permute-start.8 = (f32[80,512]{1,0:T(8,128)S(1)}, f32[80,512]{1,0:T(8,128)}, u32[]{:S(2)}, u32[]{:S(2)}) collective-permute-start(f32[80,512]{1,0:T(8,128)S(1)} %fusion.28), channel_id=1, source_target_pairs={{0,24},{8,16},{16,8},{24,0},{1,25},{9,17},{17,9},{25,1},{2,26},{10... | collective-permute-start | bytes 491528 | tf_op jit(solution)/shard_map/ppermute | solution.py:566
  535.4 31.6 %copy-start.18 = (f32[80,512]{1,0:T(8,128)}, f32[80,512]{1,0:T(8,128)S(1)}, u32[]{:S(2)}) copy-start(f32[80,512]{1,0:T(8,128)S(1)} %get-tuple-element.24) | copy-start | bytes 491524
  535.4 31.6 %copy-start.19 = (f32[80,512]{1,0:T(8,128)}, f32[80,512]{1,0:T(8,128)S(1)}, u32[]{:S(2)}) copy-start(f32[80,512]{1,0:T(8,128)S(1)} %get-tuple-element.25) | copy-start | bytes 491524
  536.9 17.0 %collective-permute-start.9 = (f32[320,512]{1,0:T(8,128)}, f32[320,512]{1,0:T(8,128)}, u32[]{:S(2)}, u32[]{:S(2)}) collective-permute-start(f32[320,512]{1,0:T(8,128)} %pad_maximum_fusion.2), channel_id=1, source_target_pairs={{0,4},{1,5},{2,6},{3,7},{4,0},{5,1},{6,2},{7,3},{8,12},{9,13},{10,... | collective-permute-start | bytes 1966088 | tf_op jit(solution)/shard_map/ppermute | solution.py:566
  537.5 17.9 %collective-permute-start.10 = (f32[320,512]{1,0:T(8,128)}, f32[320,512]{1,0:T(8,128)}, u32[]{:S(2)}, u32[]{:S(2)}) collective-permute-start(f32[320,512]{1,0:T(8,128)} %pad_maximum_fusion.2), channel_id=1, source_target_pairs={{0,2},{1,3},{2,0},{3,1},{4,6},{5,7},{6,4},{7,5},{8,10},{9,11},{10,... | collective-permute-start | bytes 1966088 | tf_op jit(solution)/shard_map/ppermute | solution.py:566
  538.9 28.1 %collective-permute-start.11 = (f32[320,512]{1,0:T(8,128)}, f32[320,512]{1,0:T(8,128)}, u32[]{:S(2)}, u32[]{:S(2)}) collective-permute-start(f32[320,512]{1,0:T(8,128)} %pad_maximum_fusion.2), channel_id=1, source_target_pairs={{0,6},{1,7},{2,4},{3,5},{4,2},{5,3},{6,0},{7,1},{8,14},{9,15},{10,... | collective-permute-start | bytes 1966088 | tf_op jit(solution)/shard_map/ppermute | solution.py:566
  545.5 21.5 %copy-start.21 = (f32[80,512]{1,0:T(8,128)S(1)}, f32[80,512]{1,0:T(8,128)}, u32[]{:S(2)}) copy-start(f32[80,512]{1,0:T(8,128)} %copy-done.20) | copy-start | bytes 491524
  545.5 21.5 %copy-start.23 = (f32[80,512]{1,0:T(8,128)S(1)}, f32[80,512]{1,0:T(8,128)}, u32[]{:S(2)}) copy-start(f32[80,512]{1,0:T(8,128)} %copy-done.22) | copy-start | bytes 491524
  572.6 26.5 %collective-permute-start.12 = (f32[1280,512]{1,0:T(8,128)}, f32[1280,512]{1,0:T(8,128)}, u32[]{:S(2)}, u32[]{:S(2)}) collective-permute-start(f32[1280,512]{1,0:T(8,128)} %pad_maximum_fusion.1), channel_id=1, source_target_pairs={{0,1},{1,0},{2,3},{3,2},{4,5},{5,4},{6,7},{7,6},{8,9},{9,8},{10,11... | collective-permute-start | bytes 7864328 | tf_op jit(solution)/shard_map/ppermute | solution.py:566
  579.2 19.9 %copy-start.14 = (f32[320,512]{1,0:T(8,128)S(1)}, f32[320,512]{1,0:T(8,128)}, u32[]{:S(2)}) copy-start(f32[320,512]{1,0:T(8,128)} %copy-done.13) | copy-start | bytes 1966084
  603.7 5.3 copy-start.10
  629.4 19.5 %copy-start.4 = (f32[6144]{0:T(1024)S(1)}, f32[6144]{0:T(1024)}, u32[]{:S(2)}) copy-start(f32[6144]{0:T(1024)} %param.4) | copy-start | bytes 73732
  (20 other events, 43.7 us)

commit v3 on v2

--- a/solution.py
+++ b/solution.py
@@ -81,6 +81,8 @@
         b1 = [bcast_lane(r1, c0 + q) for q in range(16)]
         d0 = jnp.ones((SUB, LANES), F32)
         d1 = jnp.ones((SUB, LANES), F32)
+        w0 = jnp.ones((SUB, LANES), F32)
+        w1 = jnp.ones((SUB, LANES), F32)
         for p in range(16):
             ps = p % 8
             first = p < 8
@@ -88,10 +90,12 @@
             inv = 1.0 / piv
             if first:
                 d0 = jnp.where(sub == ps, piv, d0)
+                w0 = jnp.where(sub == ps, inv, w0)
                 m0 = jnp.where(sub > ps, b0[p] * inv, 0.0)
                 m1 = b1[p] * inv
             else:
                 d1 = jnp.where(sub == ps, piv, d1)
+                w1 = jnp.where(sub == ps, inv, w1)
                 m1 = jnp.where(sub > ps, b1[p] * inv, 0.0)
             for q in range(p + 1, 16):
                 row = bcast_row(b0[q] if first else b1[q], ps)
@@ -104,14 +108,13 @@
                 e0 = e0 - m0 * re
             r1 = r1 - m1 * rr
             e1 = e1 - m1 * re
-        s0, s1 = lax.rsqrt(d0), lax.rsqrt(d1)
-        u0, u1, v0, v1 = r0 * s0, r1 * s1, e0 * s0, e1 * s1
-        out[o0], out[o1] = v0, v1
+        out[o0], out[o1] = e0 * lax.rsqrt(d0), e1 * lax.rsqrt(d1)
+        u0, u1, v0, v1 = r0 * w0, r1 * w1, e0 * w0, e1 * w1
         for o in range(2 * t + 2, octs):
             xs, ys = [], []
             for k in range(SUB):
                 i = SUB * o + k
-                g0, g1 = bcast_lane(u0, i), bcast_lane(u1, i)
+                g0, g1 = bcast_lane(r0, i), bcast_lane(r1, i)
                 xs.append(g0 * u0 + g1 * u1)
                 ys.append(g0 * v0 + g1 * v1)
             a[o] = a[o] - row_sums(xs, sub)
@@ -119,39 +122,52 @@
     return out
 
 
-def diag_kernel(lam_ref, s_ref, w_ref, work):
-    n = s_ref.shape[0]
+def open_block(work, block, lam):
+    n = work.shape[0]
+    row = lax.broadcasted_iota(jnp.int32, (n, n), 0)
+    col = lax.broadcasted_iota(jnp.int32, (n, n), 1)
+    work[:, :n] = block + jnp.where(row == col, lam, 0.0)
+    work[:, n:] = jnp.where(row == col, 1.0, 0.0)
+
+
+def eliminate(work, k):
+    n = work.shape[0]
     steps = n // BLK
     sub = lax.broadcasted_iota(jnp.int32, (SUB, LANES), 0)
     lane = lax.broadcasted_iota(jnp.int32, (SUB, LANES), 1)
-    row = lax.broadcasted_iota(jnp.int32, (n, n), 0)
-    col = lax.broadcasted_iota(jnp.int32, (n, n), 1)
-    work[:, :n] = s_ref[...] + jnp.where(row == col, lam_ref[0], 0.0)
-    work[:, n:] = jnp.where(row == col, 1.0, 0.0)
+    base = pl.multiple_of(k * BLK, BLK)
+    win = pl.ds(pl.multiple_of(base + BLK, BLK), n)
+    diag = pl.ds(base, BLK)
+
+    def load(o):
+        return work[pl.ds(pl.multiple_of(base + SUB * o, SUB), SUB), diag]
+
+    inv = jnp.concatenate(factor_block(load, sub, lane), axis=0)
+    panel = dot_cat(lhs_cat(inv), rhs_cat(work[diag, win]))
+    work[diag, win] = panel
+    right = rhs_cat(panel)
+    for j in range(steps - 1):
+        @pl.when(k == j)
+        def _(j=j):
+            rows = n - BLK * (j + 1)
+            left = lhs_cat(panel[:, :rows].T)
+            w = (pl.ds(BLK * (j + 1), rows), pl.ds(BLK * (j + 1), n))
+            work[w] = work[w] - dot_cat(left, right)
+
+
+def invert(work, block, lam):
+    open_block(work, block, lam)
 
     def step(k, carry):
-        base = pl.multiple_of(k * BLK, BLK)
-        win = pl.ds(pl.multiple_of(base + BLK, BLK), n)
-        diag = pl.ds(base, BLK)
-
-        def load(o):
-            return work[pl.ds(pl.multiple_of(base + SUB * o, SUB), SUB), diag]
-
-        inv = jnp.concatenate(factor_block(load, sub, lane), axis=0)
-        panel = dot_cat(lhs_cat(inv), rhs_cat(work[diag, win]))
-        work[diag, win] = panel
-        right = rhs_cat(panel)
-        for j in range(steps - 1):
-            @pl.when(k == j)
-            def _(j=j):
-                rows = n - BLK * (j + 1)
-                left = lhs_cat(panel[:, :rows].T)
-                w = (pl.ds(BLK * (j + 1), rows), pl.ds(BLK * (j + 1), n))
-                work[w] = work[w] - dot_cat(left, right)
+        eliminate(work, k)
         return carry
 
-    lax.fori_loop(0, steps, step, 0)
-    w_ref[...] = work[:, n:]
+    lax.fori_loop(0, work.shape[0] // BLK, step, 0)
+
+
+def diag_kernel(lam_ref, s_ref, w_ref, work):
+    invert(work, s_ref[...], lam_ref[0])
+    w_ref[...] = work[:, s_ref.shape[0]:]
 
 
 def diag_inverse(panel, lam):
@@ -168,48 +184,44 @@
     )(lam.reshape(1), panel)
 
 
-def finish_kernel(ways, h_ref, b_ref, a_hbm, *refs):
+def close_kernel(ways, lam_ref, h_ref, s_ref, a_hbm, *refs):
     n, pairs = CHUNKS, [(j, c) for c in range(CHUNKS) for j in range(c)]
-    panels, tops, inverses, refs = refs[:LAST - 1], refs[LAST - 1:2 * LAST - 1], refs[2 * LAST - 1:3 * LAST], refs[3 * LAST:]
-    x_ref, r_ref, near, a_ref, fit, load_sem, a_sem, send_sem, recv_sem = refs
+    panels, tops, inverses, refs = refs[:LAST - 1], refs[LAST - 1:2 * LAST - 1], refs[2 * LAST - 1:3 * LAST - 1], refs[3 * LAST - 1:]
+    x_ref, fit_ref, near, a_ref, work, load_sem, a_sem = refs
     hbm = [tops[j] if c == LAST else panels[j].at[:, pl.ds(NB * (c - j - 1), NB)] for j, c in pairs] + list(inverses)
-    nb = near.shape[1]
     rows_dev = a_ref.shape[0]
-    loads = [pltpu.make_async_copy(ref, near.at[i], load_sem.at[i]) for i, ref in enumerate(hbm)]
     quarter = rows_dev // a_sem.shape[0]
     spans = [pl.ds(quarter * i, quarter) for i in range(a_sem.shape[0])]
-    fetch = [pltpu.make_async_copy(a_hbm.at[span], a_ref.at[span], a_sem.at[i]) for i, span in enumerate(spans)]
-    order = [pairs.index((j, c)) if j < c else len(pairs) + c for c in range(n) for j in range(c + 1)]
-    for i in order:
-        loads[i].start()
-    for copy in fetch:
+    copies = [pltpu.make_async_copy(ref, near.at[i], load_sem.at[i]) for i, ref in enumerate(hbm)]
+    copies += [pltpu.make_async_copy(a_hbm.at[span], a_ref.at[span], a_sem.at[i]) for i, span in enumerate(spans)]
+    for copy in copies:
         copy.start()
-    z = lax.axis_index("tp")
-    barrier = pltpu.get_barrier_semaphore()
-    for m in range(1, ways):
-        pl.semaphore_signal(barrier, inc=1, device_id={"tp": z ^ m}, device_id_type=MESH)
-    pl.semaphore_wait(barrier, ways - 1)
+    invert(work, s_ref[...], lam_ref[0])
+    for copy in copies:
+        copy.wait()
 
     def upper(j, c):
         return near[pairs.index((j, c))]
+
+    def inverse(c):
+        return near[len(pairs) + c] if c < LAST else work[:, NB:]
 
     half = []
     for c in range(n):
         right = h_ref[c:c + 1, :]
         for j in range(c):
-            loads[pairs.index((j, c))].wait()
             right = right - jnp.sum(upper(j, c) * half[j], axis=0, keepdims=True)
-        loads[len(pairs) + c].wait()
-        half.append(jnp.sum(near[len(pairs) + c] * right, axis=1, keepdims=True))
+        half.append(jnp.sum(inverse(c) * right, axis=1, keepdims=True))
     for c in reversed(range(n)):
         left = half[c]
         for k in range(c + 1, n):
             left = left - jnp.sum(upper(c, k) * x_ref[k:k + 1, :], axis=1, keepdims=True)
-        x_ref[c:c + 1, :] = jnp.sum(near[len(pairs) + c] * left, axis=0, keepdims=True)
-
-    width = nb // ways
-    lanes = pl.ds(pl.multiple_of(z * width, LANES), width)
+        x_ref[c:c + 1, :] = jnp.sum(inverse(c) * left, axis=0, keepdims=True)
+
+    width = NB // ways
+    lanes = pl.ds(pl.multiple_of(lax.axis_index("tp") * width, LANES), width)
     mine = [x_ref[c:c + 1, lanes] for c in range(n)]
+    group = 4 if rows_dev % (4 * BLK) == 0 else 1
 
     def product(i, carry):
         for k in range(group):
@@ -219,21 +231,50 @@
             total = terms[0]
             for term in terms[1:]:
                 total = total + term
-            fit[z, pl.ds(at, 1), :] = jnp.sum(total.T, axis=0, keepdims=True)
+            fit_ref[pl.ds(at, 1), :] = jnp.sum(total.T, axis=0, keepdims=True)
         return carry
 
-    group = 4 if quarter % (4 * BLK) == 0 else 1
-    for i, copy in enumerate(fetch):
-        copy.wait()
-        lax.fori_loop(quarter // (group * BLK) * i, quarter // (group * BLK) * (i + 1), product, 0)
+    lax.fori_loop(0, rows_dev // (group * BLK), product, 0)
+
+
+def close(ridge, moment, corner, design_blk, uppers, tops, inverses, ways):
+    blocks = CHUNKS * (CHUNKS + 1) // 2 - 1
+    parts = [*uppers, *tops, *inverses]
+    rows_dev, cols_dev = design_blk.shape
+    smem, vmem, hbm = (pl.BlockSpec(memory_space=space) for space in (pltpu.SMEM, pltpu.VMEM, pl.ANY))
+    return pl.pallas_call(
+        functools.partial(close_kernel, ways),
+        out_shape=(jax.ShapeDtypeStruct((CHUNKS, NB), F32), jax.ShapeDtypeStruct((rows_dev // LANES, LANES), F32)),
+        in_specs=[smem, vmem, vmem, hbm] + [hbm] * len(parts),
+        out_specs=(vmem, vmem),
+        scratch_shapes=[
+            pltpu.VMEM((blocks, NB, NB), F32),
+            pltpu.VMEM((rows_dev, cols_dev), F32),
+            pltpu.VMEM((NB, 2 * NB), F32),
+            pltpu.SemaphoreType.DMA((blocks,)),
+            pltpu.SemaphoreType.DMA((4,)),
+        ],
+        compiler_params=pltpu.CompilerParams(vmem_limit_bytes=52 * 1024 * 1024),
+        cost_estimate=pl.CostEstimate(flops=25_000_000_000, bytes_accessed=32_000_000, transcendentals=0),
+        name="close",
+    )(ridge.reshape(1), moment, corner, design_blk, *parts)
+
+
+def share_kernel(ways, part_ref, b_ref, r_ref, fit, send_sem, recv_sem):
+    z = lax.axis_index("tp")
+    barrier = pltpu.get_barrier_semaphore()
+    for m in range(1, ways):
+        pl.semaphore_signal(barrier, inc=1, device_id={"tp": z ^ m}, device_id_type=MESH)
+    pl.semaphore_wait(barrier, ways - 1)
     copies = [
         pltpu.make_async_remote_copy(
-            src_ref=fit.at[z], dst_ref=fit.at[z], send_sem=send_sem.at[m - 1], recv_sem=recv_sem.at[m - 1],
+            src_ref=part_ref, dst_ref=fit.at[z], send_sem=send_sem.at[m - 1], recv_sem=recv_sem.at[m - 1],
             device_id={"tp": z ^ m}, device_id_type=MESH)
         for m in range(1, ways)
     ]
     for copy in copies:
         copy.start()
+    fit[z] = part_ref[...]
     for copy in copies:
         copy.wait()
     total = fit[0]
@@ -242,29 +283,21 @@
     r_ref[...] = b_ref[...] - total
 
 
-def finish(moment, target_blk, design_blk, uppers, tops, inverses, ways):
-    blocks = CHUNKS * (CHUNKS + 1) // 2
-    parts = [*uppers, *tops, *inverses]
-    rows_dev, cols_dev = design_blk.shape
-    vmem, hbm = pl.BlockSpec(memory_space=pltpu.VMEM), pl.BlockSpec(memory_space=pl.ANY)
+def share(part, target_blk, ways):
+    vmem = pl.BlockSpec(memory_space=pltpu.VMEM)
     return pl.pallas_call(
-        functools.partial(finish_kernel, ways),
-        out_shape=(jax.ShapeDtypeStruct((CHUNKS, NB), F32), jax.ShapeDtypeStruct((rows_dev // LANES, LANES), F32)),
-        in_specs=[vmem, vmem, hbm] + [hbm] * len(parts),
-        out_specs=(vmem, vmem),
+        functools.partial(share_kernel, ways),
+        out_shape=jax.ShapeDtypeStruct(part.shape, F32),
+        in_specs=[vmem, vmem],
+        out_specs=vmem,
         scratch_shapes=[
-            pltpu.VMEM((blocks, NB, NB), F32),
-            pltpu.VMEM((rows_dev, cols_dev), F32),
-            pltpu.VMEM((ways, rows_dev // LANES, LANES), F32),
-            pltpu.SemaphoreType.DMA((blocks,)),
-            pltpu.SemaphoreType.DMA((4,)),
+            pltpu.VMEM((ways, *part.shape), F32),
             pltpu.SemaphoreType.DMA((ways - 1,)),
             pltpu.SemaphoreType.DMA((ways - 1,)),
         ],
-        compiler_params=pltpu.CompilerParams(collective_id=1, has_side_effects=True, vmem_limit_bytes=48 * 1024 * 1024),
-        cost_estimate=pl.CostEstimate(flops=5_000_000_000, bytes_accessed=32_000_000, transcendentals=0),
-        name="finish",
-    )(moment, target_blk.reshape(-1, LANES), design_blk, *parts)
+        compiler_params=pltpu.CompilerParams(collective_id=1, has_side_effects=True),
+        name="share",
+    )(part, target_blk.reshape(part.shape))
 
 
 HIGHEST = lax.Precision.HIGHEST
@@ -632,9 +665,9 @@
             if k < PANELS - 1:
                 rest = rest[NB:] - gram(uppers[k], tops[k])
             corner = corner - gram(tops[k], tops[k])
-        inverses.append(diag_inverse(corner, ridge))
         moment = jnp.concatenate([m.reshape(1, NB) for m in moments], axis=0)
-        order, residual = finish(moment, target_blk, design_blk, uppers, tops, inverses, tp_ways)
+        order, part = close(ridge, moment, corner, design_blk, uppers, tops, inverses, tp_ways)
+        residual = share(part, target_blk, tp_ways)
         coeffs = order.reshape(CHUNKS, tp_ways, width).transpose(1, 0, 2).reshape(-1)
         return coeffs, residual.reshape(-1)
 

time: 676 us -> 668 us (0.988)
  Pallas kernels: 527 us -> 520 us
    pallas_call x5 -> x4, Pallas kernels: 98.3 us -> 78.4 us  [diag_inverse(): pl.pallas_call(diag_kernel, out_shape=jax.ShapeDtypeStruct((n, n), F32),...]
    pallas_call x1 -> x2, Pallas kernels: 16.2 us -> 29.2 us  [the longest x1 21.3 us: close(): pl.pallas_call(functools.partial(close_kernel, ways), out_shape=(jax.Shap...]
  transfers between devices with their start and end apart: 13 -> 13, of which waited for: 4 -> 5; matrix products, arithmetic and copies ran while one was open for 6% -> 7% of each run, Pallas kernels for 12% -> 12%
where the time goes in v3:
time: 668 us; the launch traced here: 661 us
  Pallas kernels  520 us (78%)
  matrix products  67.9 us (10%)
  waiting for transfers between devices  27.4 us (4%)
  starting transfers between devices  15.2 us (2%)
  local copies, waits for them, and re-layouts  14.7 us (2%)
  other arithmetic  13.5 us (2%)
    pallas_call x1, Pallas kernels, sweep(): pl.pallas_call(functools.partial(sweep_kernel, levels, tp_ways), out_shap...  412 us
    pallas_call x4, Pallas kernels, diag_inverse(): pl.pallas_call(diag_kernel, out_shape=jax.ShapeDtypeStruct((n, n), F32),...  78.4 us
    dot_general x13, matrix products, gram(): lax.dot_general(left, right, CONTRACT_ROWS, precision=HIGHEST, preferred_...  44.2 us
    ppermute x13, waiting for transfers between devices, swap(): return lax.ppermute(x, axis, [(i, i ^ mask) for i in range(ways)])  27.4 us
    pallas_call x1, Pallas kernels, close(): pl.pallas_call(functools.partial(close_kernel, ways), out_shape=(jax.Shap...  21.3 us
    dot_general x3, matrix products, local_fit(): jnp.dot(inverses[k], panels[k][:, NB:], precision=HIGHEST, preferred_elem...  16 us
    ppermute x13, starting transfers between devices, swap(): return lax.ppermute(x, axis, [(i, i ^ mask) for i in range(ways)])  15.2 us
  transfers between devices with their start and end apart: 13, of which 5 were waited for; matrix products, arithmetic and copies ran while one was open for 7% of the time, Pallas kernels for 12%

profile of v3, /device:TPU:0, one launch (start us, length us, event | category | flops | bytes accessed | tf_op | source)
XLA Modules:
  0.0 660.8 jit_solution(2112190571498930655)
XLA Ops:
  2.6 412.3 %sweep.1 = (f32[512,2048]{1,0:T(8,128)}, f32[512,1536]{1,0:T(8,128)}, f32[512,1024]{1,0:T(8,128)}, f32[512,512]{1,0:T(8,128)}, f32[1280,512]{1,0:T(8,128)}) custom-call(f32[6144,640]{1,0:T(8,128)} %a_hbm.1, f32[1536,1]{1,0:T(8,128)} %broadcast_in_dim.4.b_ref), custom_call_target="tpu_custom_call" | custom-call | flops 299999985664 | bytes 32000000 | tf_op jit(solution)/shard_map/sweep/pallas_call | solution.py:572
  414.9 2.8 dynamic-slice_bitcast_fusion.2
  421.9 19.5 %diag_inverse.4.refs_7_ = f32[512,512]{1,0:T(8,128)} custom-call(f32[1]{0:T(128)} %bitcast.81.lam_ref, f32[512,2048]{1,0:T(8,128)} %get-tuple-element.9.s_ref), custom_call_target="tpu_custom_call" | custom-call | flops 20000000000 | bytes 2097152 | tf_op jit(solution)/shard_map/diag_inverse/pallas_call | solution.py:175
  441.4 7.4 %fusion.1.refs_0_ = f32[512,1536]{1,0:T(8,128)S(1)} fusion(f32[512,512]{1,0:T(8,128)} %diag_inverse.4.refs_7_, f32[512,2048]{1,0:T(8,128)} %get-tuple-element.9.s_ref), kind=kOutput, calls=%fused_computation.3 | convolution fusion | flops 4831838208 | bytes 7340032 | tf_op jit(solution)/shard_map/dot_general | solution.py:654
  448.9 9.4 %convolution_subtract_fusion.s_ref = f32[512,1536]{1,0:T(8,128)} fusion(f32[512,1536]{1,0:T(8,128)} %get-tuple-element.10, f32[512,1536]{1,0:T(8,128)S(1)} %fusion.1.refs_0_), kind=kOutput, calls=%fused_computation | convolution fusion | flops 4832624640 | bytes 10485760 | tf_op jit(solution)/shard_map/dot_general | solution.py:308
  458.3 19.7 %diag_inverse.5.refs_8_ = f32[512,512]{1,0:T(8,128)} custom-call(f32[1]{0:T(128)} %bitcast.82.lam_ref, f32[512,1536]{1,0:T(8,128)} %convolution_subtract_fusion.s_ref), custom_call_target="tpu_custom_call" | custom-call | flops 20000000000 | bytes 2097152 | tf_op jit(solution)/shard_map/diag_inverse/pallas_call | solution.py:175
  478.0 5.5 fusion.3.refs_1_
  483.5 3.6 fusion.14
  491.9 2.7 collective-permute-start.5
  494.6 5.0 subtract_subtract_fusion.s_ref
  499.6 4.0 collective-permute-done.5
  503.6 5.4 collective-permute-done.4
  514.5 19.5 %diag_inverse.6.refs_9_ = f32[512,512]{1,0:T(8,128)} custom-call(f32[1]{0:T(128)} %bitcast.83.lam_ref, f32[512,1024]{1,0:T(8,128)} %subtract_subtract_fusion.s_ref), custom_call_target="tpu_custom_call" | custom-call | flops 20000000000 | bytes 2097152 | tf_op jit(solution)/shard_map/diag_inverse/pallas_call | solution.py:175
  543.3 3.1 fusion.10.refs_2_
  546.5 2.8 convolution_subtract_fusion.3
  549.3 7.0 %collective-permute-done.11 = f32[320,512]{1,0:T(8,128)} collective-permute-done((f32[320,512]{1,0:T(8,128)}, f32[320,512]{1,0:T(8,128)}, u32[]{:S(2)}, u32[]{:S(2)}) %collective-permute-start.11) | collective-permute-done | bytes 655392 | tf_op jit(solution)/shard_map/ppermute | solution.py:599
  556.3 10.0 %collective-permute-done.10 = f32[320,512]{1,0:T(8,128)} collective-permute-done((f32[320,512]{1,0:T(8,128)}, f32[320,512]{1,0:T(8,128)}, u32[]{:S(2)}, u32[]{:S(2)}) %collective-permute-start.10) | collective-permute-done | bytes 655392 | tf_op jit(solution)/shard_map/ppermute | solution.py:599
  576.7 2.8 convolution_subtract_fusion.1.s_ref
  579.5 19.8 %diag_inverse.7.refs_10_ = f32[512,512]{1,0:T(8,128)} custom-call(f32[1]{0:T(128)} %bitcast.84.lam_ref, f32[512,512]{1,0:T(8,128)} %convolution_subtract_fusion.1.s_ref), custom_call_target="tpu_custom_call" | custom-call | flops 20000000000 | bytes 2097152 | tf_op jit(solution)/shard_map/diag_inverse/pallas_call | solution.py:175
  599.3 2.8 broadcast_select_fusion
  604.0 5.3 fusion
  611.2 3.8 slice_subtract_fusion
  628.8 21.3 %close.1 = (f32[5,512]{1,0:T(8,128)S(1)}, f32[48,128]{1,0:T(8,128)S(1)}) custom-call(f32[1]{0:T(128)} %bitcast.85.lam_ref, f32[5,512]{1,0:T(8,128)S(1)} %concatenate.14.h_ref, f32[512,512]{1,0:T(8,128)S(1)} %fusion.24.s_ref, f32[6144,640]{1,0:T(8,128)} %a_hbm.1, f32[512,1536]{1,0:T(8,128)} %copy-done.1, f32[512,1024]{1,0:T(8,128)} %copy-done.3, ...), custom_call_target="tpu_custom_call" | custom-call | flops 24999999488 | bytes 32000000 | tf_op jit(solution)/shard_map/close/pallas_call | solution.py:245
  651.3 7.9 %share.1 = f32[48,128]{1,0:T(8,128)} custom-call(f32[48,128]{1,0:T(8,128)} %copy-done, f32[48,128]{1,0:T(8,128)} %bitcast.92), custom_call_target="tpu_custom_call" | custom-call | tf_op jit(solution)/shard_map/share/pallas_call | solution.py:288
  (116 shorter events, 55.3 us)
Async XLA Ops:
  417.8 69.3 %collective-permute-start = (f32[320,512]{1,0:T(8,128)}, f32[320,512]{1,0:T(8,128)}, u32[]{:S(2)}, u32[]{:S(2)}) collective-permute-start(f32[320,512]{1,0:T(8,128)} %get-tuple-element.21), channel_id=1, source_target_pairs={{0,2},{1,3},{2,0},{3,1},{4,6},{5,7},{6,4},{7,5},{8,10},{9,11},{10,... | collective-permute-start | bytes 1966088 | tf_op jit(solution)/shard_map/ppermute | solution.py:599
  418.4 68.7 %collective-permute-start.2 = (f32[320,512]{1,0:T(8,128)}, f32[320,512]{1,0:T(8,128)}, u32[]{:S(2)}, u32[]{:S(2)}) collective-permute-start(f32[320,512]{1,0:T(8,128)} %get-tuple-element.22), channel_id=1, source_target_pairs={{0,6},{1,7},{2,4},{3,5},{4,2},{5,3},{6,0},{7,1},{8,14},{9,15},{10,... | collective-permute-start | bytes 1966088 | tf_op jit(solution)/shard_map/ppermute | solution.py:599
  420.1 67.0 %collective-permute-start.1 = (f32[320,512]{1,0:T(8,128)}, f32[320,512]{1,0:T(8,128)}, u32[]{:S(2)}, u32[]{:S(2)}) collective-permute-start(f32[320,512]{1,0:T(8,128)} %get-tuple-element.23), channel_id=1, source_target_pairs={{0,4},{1,5},{2,6},{3,7},{4,0},{5,1},{6,2},{7,3},{8,12},{9,13},{10,... | collective-permute-start | bytes 1966088 | tf_op jit(solution)/shard_map/ppermute | solution.py:599
  448.8 92.9 %copy-start.1 = (f32[512,1536]{1,0:T(8,128)}, f32[512,1536]{1,0:T(8,128)S(1)}, u32[]{:S(2)}) copy-start(f32[512,1536]{1,0:T(8,128)S(1)} %fusion.1.refs_0_) | copy-start | bytes 9437188
  487.1 7.5 %copy-start.25 = (f32[512,1024]{1,0:T(8,128)S(1)}, f32[512,1024]{1,0:T(8,128)}, u32[]{:S(2)}) copy-start(f32[512,1024]{1,0:T(8,128)} %get-tuple-element.11) | copy-start | bytes 6291460
  490.9 8.7 %collective-permute-start.3 = (f32[80,512]{1,0:T(8,128)}, f32[80,512]{1,0:T(8,128)S(1)}, u32[]{:S(2)}, u32[]{:S(2)}) collective-permute-start(f32[80,512]{1,0:T(8,128)} %get-tuple-element.28), channel_id=1, source_target_pairs={{0,8},{8,0},{16,24},{24,16},{1,9},{9,1},{17,25},{25,17},{2,10},{10... | collective-permute-start | bytes 491528 | tf_op jit(solution)/shard_map/ppermute | solution.py:599
  491.9 11.7 %collective-permute-start.5 = (f32[80,512]{1,0:T(8,128)}, f32[80,512]{1,0:T(8,128)}, u32[]{:S(2)}, u32[]{:S(2)}) collective-permute-start(f32[80,512]{1,0:T(8,128)} %get-tuple-element.29), channel_id=1, source_target_pairs={{0,24},{8,16},{16,8},{24,0},{1,25},{9,17},{17,9},{25,1},{2,26},{10... | collective-permute-start | bytes 491528 | tf_op jit(solution)/shard_map/ppermute | solution.py:599
  494.6 14.3 %collective-permute-start.4 = (f32[80,512]{1,0:T(8,128)S(1)}, f32[80,512]{1,0:T(8,128)}, u32[]{:S(2)}, u32[]{:S(2)}) collective-permute-start(f32[80,512]{1,0:T(8,128)S(1)} %get-tuple-element.30), channel_id=1, source_target_pairs={{0,16},{8,24},{16,0},{24,8},{1,17},{9,25},{17,1},{25,9},{2,18},{10... | collective-permute-start | bytes 491528 | tf_op jit(solution)/shard_map/ppermute | solution.py:599
  510.1 24.0 %copy-start.28 = (f32[80,512]{1,0:T(8,128)}, f32[80,512]{1,0:T(8,128)S(1)}, u32[]{:S(2)}) copy-start(f32[80,512]{1,0:T(8,128)S(1)} %fusion.28) | copy-start | bytes 491524
  510.1 24.0 %collective-permute-start.8 = (f32[80,512]{1,0:T(8,128)S(1)}, f32[80,512]{1,0:T(8,128)S(1)}, u32[]{:S(2)}, u32[]{:S(2)}) collective-permute-start(f32[80,512]{1,0:T(8,128)S(1)} %fusion.28), channel_id=1, source_target_pairs={{0,24},{8,16},{16,8},{24,0},{1,25},{9,17},{17,9},{25,1},{2,26},{10... | collective-permute-start | bytes 491528 | tf_op jit(solution)/shard_map/ppermute | solution.py:599
  512.8 21.3 %collective-permute-start.7 = (f32[80,512]{1,0:T(8,128)S(1)}, f32[80,512]{1,0:T(8,128)}, u32[]{:S(2)}, u32[]{:S(2)}) collective-permute-start(f32[80,512]{1,0:T(8,128)S(1)} %fusion.28), channel_id=1, source_target_pairs={{0,8},{8,0},{16,24},{24,16},{1,9},{9,1},{17,25},{25,17},{2,10},{10... | collective-permute-start | bytes 491528 | tf_op jit(solution)/shard_map/ppermute | solution.py:599
  512.8 21.9 %collective-permute-start.6 = (f32[80,512]{1,0:T(8,128)S(1)}, f32[80,512]{1,0:T(8,128)}, u32[]{:S(2)}, u32[]{:S(2)}) collective-permute-start(f32[80,512]{1,0:T(8,128)S(1)} %fusion.28), channel_id=1, source_target_pairs={{0,16},{8,24},{16,0},{24,8},{1,17},{9,25},{17,1},{25,9},{2,18},{10... | collective-permute-start | bytes 491528 | tf_op jit(solution)/shard_map/ppermute | solution.py:599
  536.0 31.4 %copy-start.18 = (f32[80,512]{1,0:T(8,128)}, f32[80,512]{1,0:T(8,128)S(1)}, u32[]{:S(2)}) copy-start(f32[80,512]{1,0:T(8,128)S(1)} %get-tuple-element.24) | copy-start | bytes 491524
  536.0 31.4 %copy-start.19 = (f32[80,512]{1,0:T(8,128)}, f32[80,512]{1,0:T(8,128)S(1)}, u32[]{:S(2)}) copy-start(f32[80,512]{1,0:T(8,128)S(1)} %get-tuple-element.25) | copy-start | bytes 491524
  537.5 18.8 %collective-permute-start.11 = (f32[320,512]{1,0:T(8,128)}, f32[320,512]{1,0:T(8,128)}, u32[]{:S(2)}, u32[]{:S(2)}) collective-permute-start(f32[320,512]{1,0:T(8,128)} %pad_maximum_fusion.2), channel_id=1, source_target_pairs={{0,6},{1,7},{2,4},{3,5},{4,2},{5,3},{6,0},{7,1},{8,14},{9,15},{10,... | collective-permute-start | bytes 1966088 | tf_op jit(solution)/shard_map/ppermute | solution.py:599
  538.8 27.5 %collective-permute-start.10 = (f32[320,512]{1,0:T(8,128)}, f32[320,512]{1,0:T(8,128)}, u32[]{:S(2)}, u32[]{:S(2)}) collective-permute-start(f32[320,512]{1,0:T(8,128)} %pad_maximum_fusion.2), channel_id=1, source_target_pairs={{0,2},{1,3},{2,0},{3,1},{4,6},{5,7},{6,4},{7,5},{8,10},{9,11},{10,... | collective-permute-start | bytes 1966088 | tf_op jit(solution)/shard_map/ppermute | solution.py:599
  539.4 27.9 %collective-permute-start.9 = (f32[320,512]{1,0:T(8,128)}, f32[320,512]{1,0:T(8,128)}, u32[]{:S(2)}, u32[]{:S(2)}) collective-permute-start(f32[320,512]{1,0:T(8,128)} %pad_maximum_fusion.2), channel_id=1, source_target_pairs={{0,4},{1,5},{2,6},{3,7},{4,0},{5,1},{6,2},{7,3},{8,12},{9,13},{10,... | collective-permute-start | bytes 1966088 | tf_op jit(solution)/shard_map/ppermute | solution.py:599
  546.5 70.4 %copy-start.5 = (f32[512,512]{1,0:T(8,128)}, f32[512,512]{1,0:T(8,128)S(1)}, u32[]{:S(2)}) copy-start(f32[512,512]{1,0:T(8,128)S(1)} %fusion.10.refs_2_) | copy-start | bytes 3145732
  546.5 20.9 %copy-start.21 = (f32[80,512]{1,0:T(8,128)S(1)}, f32[80,512]{1,0:T(8,128)}, u32[]{:S(2)}) copy-start(f32[80,512]{1,0:T(8,128)} %copy-done.20) | copy-start | bytes 491524
  546.5 20.9 %copy-start.23 = (f32[80,512]{1,0:T(8,128)S(1)}, f32[80,512]{1,0:T(8,128)}, u32[]{:S(2)}) copy-start(f32[80,512]{1,0:T(8,128)} %copy-done.22) | copy-start | bytes 491524
  572.9 26.4 %collective-permute-start.12 = (f32[1280,512]{1,0:T(8,128)}, f32[1280,512]{1,0:T(8,128)}, u32[]{:S(2)}, u32[]{:S(2)}) collective-permute-start(f32[1280,512]{1,0:T(8,128)} %pad_maximum_fusion.1), channel_id=1, source_target_pairs={{0,1},{1,0},{2,3},{3,2},{4,5},{5,4},{6,7},{7,6},{8,9},{9,8},{10,11... | collective-permute-start | bytes 7864328 | tf_op jit(solution)/shard_map/ppermute | solution.py:599
  579.5 19.8 %copy-start.11 = (f32[320,512]{1,0:T(8,128)S(1)}, f32[320,512]{1,0:T(8,128)}, u32[]{:S(2)}) copy-start(f32[320,512]{1,0:T(8,128)} %copy-done.10) | copy-start | bytes 1966084
  604.0 18.5 %copy-start.6 = (f32[512,512]{1,0:T(8,128)}, f32[512,512]{1,0:T(8,128)S(1)}, u32[]{:S(2)}) copy-start(f32[512,512]{1,0:T(8,128)S(1)} %fusion.20.refs_3_) | copy-start | bytes 3145732
  611.2 9.4 %copy-start.7 = (f32[512,512]{1,0:T(8,128)}, f32[512,512]{1,0:T(8,128)S(1)}, u32[]{:S(2)}) copy-start(f32[512,512]{1,0:T(8,128)S(1)} %fusion.17.refs_4_) | copy-start | bytes 3145732
  (21 other events, 52.7 us)
